TPU v7x, 32 devices: a 4x4x1 block of a 4x4x8 slice. The times are simulated.
32 devices in a mesh: dp: 1 (over z), tp: 32 (over y, x, core).
Axes of the slice: x: 4, y: 4, z: 1, core: 2. Of those that a mesh axis runs over, the one named last changes fastest.
The devices are a block of a 4x4x8 slice.
Arguments:
- x_in: bfloat16 [2048, 8192], P(('dp', 'tp'))
- dy_in: bfloat16 [2048, 8192], P(('dp', 'tp'))
- w_q: bfloat16 [8192, 128, 64], P(None, 'tp')
- w_k: bfloat16 [8192, 8, 64], replicated
- w_v: bfloat16 [8192, 8, 64], replicated
- w_o: bfloat16 [128, 64, 8192], P('tp')
Outputs:
- output 1: bfloat16 [2048, 8192], P(('dp', 'tp'))
- output 2: float32 [8192, 128, 64], P('dp', 'tp')
- output 3: float32 [128, 64, 8192], P(('dp', 'tp'))
- output 4: float32 [65536, 64], P(('dp', 'tp'))
- output 5: float32 [65536, 64], P(('dp', 'tp'))
All inputs are finite; a program needn't handle non-finite values.
Results may differ from a plain program's by a relative error of at most 0.00953466.
Values are sent between devices in bfloat16 or wider.
A program may use at most 768 MiB of HBM per device.

v0:
```python
import jax
import jax.numpy as jnp
from jax import lax
from jax.sharding import PartitionSpec as P


def solution(mesh):
    n_model = mesh.shape["tp"]

    def local_grads(x_blk, dy_blk, wq_loc, w_k, w_v, wo_loc):
        f32 = jnp.float32
        bf16 = jnp.bfloat16
        model_dim, kv_heads, head_dim = w_k.shape
        repl = n_model // kv_heads
        scale = head_dim ** -0.5
        dev_idx = lax.axis_index("tp")
        kv_index = dev_idx // repl
        wk_loc = lax.dynamic_index_in_dim(w_k, kv_index, axis=1, keepdims=False)
        wv_loc = lax.dynamic_index_in_dim(w_v, kv_index, axis=1, keepdims=False)
        x_full = lax.all_gather(x_blk, "tp", axis=0, tiled=True)
        dy_full = lax.all_gather(dy_blk, "tp", axis=0, tiled=True)
        tokens = x_full.shape[0]
        queries = jnp.einsum("tc,che->hte", x_full, wq_loc, preferred_element_type=f32).astype(bf16)
        key_rows = jnp.dot(x_full, wk_loc, preferred_element_type=f32).astype(bf16)
        val_rows = jnp.dot(x_full, wv_loc, preferred_element_type=f32).astype(bf16)
        causal = lax.broadcasted_iota(jnp.int32, (tokens, tokens), 0) >= lax.broadcasted_iota(jnp.int32, (tokens, tokens), 1)
        scores = jnp.einsum("hqe,ke->hqk", queries, key_rows, preferred_element_type=f32) * scale
        scores = jnp.where(causal, scores, -jnp.inf)
        attn_prob = jax.nn.softmax(scores, axis=-1)
        prob_bf = attn_prob.astype(bf16)
        attn_out = jnp.einsum("hqk,ke->hqe", prob_bf, val_rows, preferred_element_type=f32).astype(bf16)
        d_out = jnp.einsum("tc,hec->hte", dy_full, wo_loc, preferred_element_type=f32).astype(bf16)
        grad_wo = jnp.einsum("hte,tc->hec", attn_out, dy_full, preferred_element_type=f32)
        d_prob = jnp.einsum("hqe,ke->hqk", d_out, val_rows, preferred_element_type=f32)
        delta_row = jnp.einsum("hqe,hqe->hq", d_out, attn_out, preferred_element_type=f32)[..., None]
        d_score = (attn_prob * (d_prob - delta_row)).astype(bf16)
        d_query = (jnp.einsum("hqk,ke->hqe", d_score, key_rows, preferred_element_type=f32) * scale).astype(bf16)
        d_key = (jnp.einsum("hqk,hqe->ke", d_score, queries, preferred_element_type=f32) * scale).astype(bf16)
        d_val = jnp.einsum("hqk,hqe->ke", prob_bf, d_out, preferred_element_type=f32).astype(bf16)
        grad_wq = jnp.einsum("tc,hte->che", x_full, d_query, preferred_element_type=f32)
        dx_part = (jnp.einsum("hte,che->tc", d_query, wq_loc, preferred_element_type=f32)
                   + jnp.einsum("te,ce->tc", d_key, wk_loc, preferred_element_type=f32)
                   + jnp.einsum("te,ce->tc", d_val, wv_loc, preferred_element_type=f32))
        dx_blk = lax.psum_scatter(dx_part, "tp", scatter_dimension=0, tiled=True).astype(bf16)
        slot = (jnp.arange(kv_heads) == kv_index)[:, None, None]
        wk_part = jnp.einsum("tc,te->ce", x_full, d_key, preferred_element_type=f32)
        wv_part = jnp.einsum("tc,te->ce", x_full, d_val, preferred_element_type=f32)
        wk_buf = jnp.where(slot, wk_part[None], 0.0).reshape(kv_heads * model_dim, head_dim)
        wv_buf = jnp.where(slot, wv_part[None], 0.0).reshape(kv_heads * model_dim, head_dim)
        dwk_blk = lax.psum_scatter(wk_buf, "tp", scatter_dimension=0, tiled=True)
        dwv_blk = lax.psum_scatter(wv_buf, "tp", scatter_dimension=0, tiled=True)
        return dx_blk, grad_wq, grad_wo, dwk_blk, dwv_blk

    tok_spec = P(("dp", "tp"))
    return jax.shard_map(
        local_grads,
        mesh=mesh,
        in_specs=(tok_spec, tok_spec, P(None, "tp", None), P(), P(), P("tp")),
        out_specs=(tok_spec, P("dp", "tp", None), tok_spec, tok_spec, tok_spec),
        check_vma=False,
    )
```

profile of v0, /device:TPU:97, one launch (start us, length us, event | category | flops | bytes accessed | tf_op | source)
XLA Modules:
  0.0 974.0 jit_solution(5444344810631188131)
XLA Ops:
  7.2 0.1 all-gather.3.cloned.1.call-start
  7.2 0.7 all-gather.3.cloned.1.call-update
  8.0 0.1 all-gather.5.cloned.1.call-start
  8.0 0.7 all-gather.5.cloned.1.call-update
  8.8 0.1 reduce-scatter.4.cloned.1.call-start
  8.9 4.1 iota_compare_fusion
  13.0 109.6 %all-gather.3.cloned.1.call-done = bf16[2048,8192]{1,0:T(8,128)(2,1)} async-done(((bf16[64,8192]{1,0:T(8,128)(2,1)}), bf16[2048,8192]{1,0:T(8,128)(2,1)}) %all-gather.3.cloned.1.call-update) | async-done | bytes 33554448 | tf_op jit(solution)/shard_map/all_gather | solution.py:20
  122.6 15.7 %fusion.37 = bf16[64,2048,1]{1,0,2:T(8,128)(2,1)S(1)} fusion(bf16[2048,8192]{1,0:T(8,128)(2,1)} %all-gather.3.cloned.1.call-done, bf16[8192,8,64]{0,2,1:T(8,128)(2,1)} %param.10, s32[]{:T(128)S(6)} %select_n.24), kind=kOutput, calls=%fused_computation.42 | convolution fusion | flops 2147614720 | bytes 34865156 | tf_op jit(solution)/shard_map/dot_general | solution.py:25
  138.3 15.7 %fusion.36 = bf16[64,2048,1]{1,0,2:T(8,128)(2,1)S(1)} fusion(bf16[2048,8192]{1,0:T(8,128)(2,1)} %all-gather.3.cloned.1.call-done, bf16[8192,8,64]{0,2,1:T(8,128)(2,1)} %param.9, s32[]{:T(128)S(6)} %select_n.24), kind=kOutput, calls=%fused_computation.41 | convolution fusion | flops 2147614720 | bytes 34865156 | tf_op jit(solution)/shard_map/dot_general | solution.py:24
  154.0 0.0 copy-start.4
  154.0 15.8 %fusion.30 = bf16[4,2048,64]{1,2,0:T(8,128)(2,1)S(1)} fusion(bf16[8192,4,64]{0,2,1:T(8,128)(2,1)} %param.8, bf16[2048,8192]{1,0:T(8,128)(2,1)} %all-gather.3.cloned.1.call-done), kind=kOutput, calls=%fused_computation.33 | convolution fusion | flops 8590458880 | bytes 38797312 | tf_op jit(solution)/shard_map/tc,che->hte/dot_general | solution.py:23
  169.8 0.0 copy-done.4
  169.8 0.0 copy-start.6
  169.8 31.6 %fusion.55 = (f32[4,2048]{1,0:T(4,128)S(1)}, f32[4,2048,2048]{1,2,0:T(8,128)}) fusion(pred[2048,2048]{0,1:T(8,128)(4,1)} %iota_compare_fusion, bf16[4,2048,64]{1,2,0:T(8,128)(2,1)S(1)} %fusion.30, bf16[64,2048,1]{1,0,2:T(8,128)(2,1)S(1)} %fusion.36), kind=kOutput, calls=%fused_computation.63 | convolution fusion | flops 2214594560 | bytes 72646656 | tf_op jit(solution)/shard_map/sub | solution.py:29
  201.5 0.0 copy-done.6
  201.5 32.8 %fusion.14 = bf16[4,2048,2048]{1,2,0:T(8,128)(2,1)} fusion(f32[4,2048,2048]{1,2,0:T(8,128)} %get-tuple-element.8, f32[4,2048]{1,0:T(4,128)S(1)} %get-tuple-element.7), kind=kLoop, calls=%fused_computation.19 | loop fusion | flops 33554432 | bytes 100696064 | tf_op jit(solution)/shard_map/convert_element_type | solution.py:30
  234.2 14.1 %convolution_convert_fusion = bf16[4,2048,64]{1,2,0:T(8,128)(2,1)S(1)} fusion(bf16[64,2048,1]{1,0,2:T(8,128)(2,1)S(1)} %fusion.37, bf16[4,2048,2048]{1,2,0:T(8,128)(2,1)} %fusion.14), kind=kOutput, calls=%fused_computation.31 | convolution fusion | flops 2148007936 | bytes 34865152 | tf_op jit(solution)/shard_map/hqk,ke->hqe/dot_general | solution.py:31
  248.4 0.0 copy-start
  248.4 0.0 all-gather.5.cloned.1.call-done
  248.4 16.2 %fusion.38 = (f32[4,2048]{1,0:T(4,128)S(1)}, bf16[4,2048,64]{1,2,0:T(8,128)(2,1)S(1)}) fusion(bf16[4,2048,64]{1,2,0:T(8,128)(2,1)S(1)} %convolution_convert_fusion, bf16[4,64,8192]{2,1,0:T(8,128)(2,1)} %param.11, bf16[2048,8192]{1,0:T(8,128)(2,1)} %all-gather.5.cloned.1.call-done), kind=kOutput, calls=%fused_computation.44 | convolution fusion | flops 8592547840 | bytes 39878656 | tf_op jit(solution)/shard_map/tc,hec->hte/dot_general | solution.py:32
  264.7 0.0 copy-start.8
  264.7 16.6 %fusion.35 = bf16[2048,64]{0,1:T(8,128)(2,1)S(1)} fusion(bf16[4,2048,2048]{1,2,0:T(8,128)(2,1)} %fusion.14, bf16[4,2048,64]{1,2,0:T(8,128)(2,1)S(1)} %get-tuple-element.10), kind=kOutput, calls=%fused_computation.38 | convolution fusion | flops 2147614720 | bytes 34865152 | tf_op jit(solution)/shard_map/hqk,hqe->ke/dot_general | solution.py:39
  281.3 0.0 copy-done
  281.3 0.0 copy-done.8
  281.3 0.0 copy-start.7
  281.3 36.0 %multiply_convert_fusion = bf16[4,2048,2048]{1,2,0:T(8,128)(2,1)} fusion(bf16[4,2048,64]{1,2,0:T(8,128)(2,1)} %copy-done.8, bf16[64,2048,1]{1,0,2:T(8,128)(2,1)S(1)} %fusion.37, f32[4,2048]{1,0:T(4,128)S(1)} %get-tuple-element.9, f32[4,2048,2048]{1,2,0:T(8,128)} %get-tuple-element.8, f32[4,2048]{1,0:T(4,128)S(1)} %get-tuple-element.7), kind=kOutput, calls=%fused_computation.3 | convolution fusion | flops 2214592512 | bytes 102039552 | tf_op jit(solution)/shard_map/hqe,ke->hqk/dot_general | solution.py:34
  317.3 0.0 copy-done.7
  317.3 0.0 copy-start.5
  317.3 16.4 %fusion.34 = bf16[2048,64]{0,1:T(8,128)(2,1)S(1)} fusion(bf16[4,2048,2048]{1,2,0:T(8,128)(2,1)} %multiply_convert_fusion, bf16[4,2048,64]{1,2,0:T(8,128)(2,1)S(1)} %copy-done.7), kind=kOutput, calls=%fused_computation.37 | convolution fusion | flops 2147745792 | bytes 34865152 | tf_op jit(solution)/shard_map/hqk,hqe->ke/dot_general | solution.py:38
  333.7 0.0 copy-done.5
  333.7 0.0 copy-start.2
  333.7 13.8 %fusion.20 = bf16[4,2048,64]{1,2,0:T(8,128)(2,1)S(1)} fusion(bf16[64,2048,1]{1,0,2:T(8,128)(2,1)S(1)} %copy-done.5, bf16[4,2048,2048]{1,2,0:T(8,128)(2,1)} %multiply_convert_fusion), kind=kOutput, calls=%fused_computation.28 | convolution fusion | flops 2148532224 | bytes 34865152 | tf_op jit(solution)/shard_map/hqk,ke->hqe/dot_general | solution.py:37
  347.5 24.4 %fusion.39 = f32[2048,8192]{1,0:T(8,128)} fusion(bf16[2048,64]{0,1:T(8,128)(2,1)S(1)} %fusion.35, bf16[8192,8,64]{0,2,1:T(8,128)(2,1)} %param.10, s32[]{:T(128)S(6)} %select_n.24), kind=kOutput, calls=%fused_computation.45 | convolution fusion | flops 2147483648 | bytes 68419584 | tf_op jit(solution)/shard_map/te,ce->tc/dot_general | solution.py:43
  371.9 0.0 copy-done.2
  371.9 24.4 %fusion.42 = f32[2048,8192]{1,0:T(8,128)} fusion(bf16[2048,64]{0,1:T(8,128)(2,1)S(1)} %fusion.34, bf16[8192,8,64]{0,2,1:T(8,128)(2,1)} %param.9, s32[]{:T(128)S(6)} %select_n.24), kind=kOutput, calls=%fused_computation.48 | convolution fusion | flops 2147483648 | bytes 68419584 | tf_op jit(solution)/shard_map/te,ce->tc/dot_general | solution.py:42
  396.3 66.4 %fusion.1 = f32[2048,8192]{1,0:T(8,128)} fusion(f32[2048,8192]{1,0:T(8,128)} %fusion.39, f32[2048,8192]{1,0:T(8,128)} %fusion.42, bf16[4,2048,64]{1,2,0:T(8,128)(2,1)S(1)} %fusion.20, bf16[8192,4,64]{0,2,1:T(8,128)(2,1)} %param.8), kind=kOutput, calls=%fused_computation.2 | convolution fusion | flops 8623489024 | bytes 206569472 | tf_op jit(solution)/shard_map/hte,che->tc/dot_general | solution.py:41
  462.6 0.1 reduce-scatter.4.cloned.1.call-update
  462.7 0.1 reduce-scatter.8.cloned.1.call-start
  462.8 0.1 broadcast_bitcast_fusion
  462.9 13.8 %convolution_bitcast_fusion = f32[8192,64]{0,1:T(8,128)S(1)} fusion(bf16[2048,64]{0,1:T(8,128)(2,1)S(1)} %fusion.35, bf16[2048,8192]{1,0:T(8,128)(2,1)} %all-gather.3.cloned.1.call-done), kind=kOutput, calls=%fused_computation.22 | convolution fusion | flops 2147483648 | bytes 35913728 | tf_op jit(solution)/shard_map/tc,te->ce/dot_general | solution.py:47
  476.7 0.0 copy-start.3
  476.7 7.8 broadcast_in_dim.59
  484.5 17.7 %copy.28 = f32[8,8,8,8192]{3,1,2,0:T(8,128)} copy(f32[8,8,8,8192]{3,2,1,0:T(8,128)} %bitcast.103) | data formatting | bytes 33554432
  502.2 0.0 copy-done.3
  502.2 13.6 %convolution_bitcast_fusion.1 = f32[8192,64]{0,1:T(8,128)S(1)} fusion(bf16[2048,64]{0,1:T(8,128)(2,1)S(1)} %copy-done.3, bf16[2048,8192]{1,0:T(8,128)(2,1)} %all-gather.3.cloned.1.call-done), kind=kOutput, calls=%fused_computation.23 | convolution fusion | flops 2147483648 | bytes 35913728 | tf_op jit(solution)/shard_map/tc,te->ce/dot_general | solution.py:46
  515.8 7.8 broadcast_in_dim.56
  523.5 0.0 slice-start
  523.5 0.0 slice-start.1
  523.5 20.9 %copy.27 = f32[8,8,8,8192]{3,1,2,0:T(8,128)} copy(f32[8,8,8,8192]{3,2,1,0:T(8,128)} %bitcast.104) | data formatting | bytes 33554432
  544.4 0.0 slice-done
  544.4 0.0 slice-done.1
  544.5 0.0 slice-done.2
  544.5 0.0 slice-done.3
  544.5 16.5 %broadcast_select_fusion = (f32[65536,64]{0,1:T(8,128)}, f32[65536,64]{0,1:T(8,128)}) fusion(f32[65536,64]{0,1:T(8,128)S(1)} %bitcast.101, pred[65536]{0:T(1024)(128)(4,1)S(1)} %bitcast.105, f32[65536,64]{0,1:T(8,128)} %bitcast.102), kind=kLoop, calls=%fused_computation.24 | loop fusion | flops 8388608 | bytes 67174400 | tf_op jit(solution)/shard_map/jit(_where)/select_n | solution.py:49
  561.0 0.1 reduce-scatter.8.cloned.1.call-update
  561.0 0.1 reduce-scatter.6.cloned.1.call-start
  561.1 0.6 reduce-scatter.6.cloned.1.call-update
  561.7 0.5 copy-done.1
  562.2 17.1 %fusion.3 = f32[4,64,8192]{2,1,0:T(8,128)} fusion(bf16[4,2048,64]{1,2,0:T(8,128)(2,1)S(1)} %copy-done.1, bf16[2048,8192]{1,0:T(8,128)(2,1)} %all-gather.5.cloned.1.call-done), kind=kOutput, calls=%fused_computation.7 | convolution fusion | flops 8589934592 | bytes 42991616 | tf_op jit(solution)/shard_map/hte,tc->hec/dot_general | solution.py:33
  579.3 17.1 %fusion.15 = f32[8192,4,64]{0,2,1:T(8,128)} fusion(bf16[4,2048,64]{1,2,0:T(8,128)(2,1)S(1)} %fusion.20, bf16[2048,8192]{1,0:T(8,128)(2,1)} %all-gather.3.cloned.1.call-done), kind=kOutput, calls=%fused_computation.21 | convolution fusion | flops 8589934592 | bytes 42991616 | tf_op jit(solution)/shard_map/tc,hte->che/dot_general | solution.py:40
  596.3 149.7 %reduce-scatter.4.cloned.1.call-done = f32[64,8192]{1,0:T(8,128)} async-done(((f32[2048,8192]{1,0:T(8,128)}), f32[64,8192]{1,0:T(8,128)}) %reduce-scatter.4.cloned.1.call-update) | async-done | bytes 2097168 | tf_op jit(solution)/shard_map/reduce_scatter | solution.py:44
  746.0 2.7 convert_element_type.53
  748.7 107.3 %reduce-scatter.8.cloned.1.call-done = f32[2048,64]{0,1:T(8,128)} async-done(((f32[65536,64]{0,1:T(8,128)}), f32[2048,64]{0,1:T(8,128)}) %reduce-scatter.8.cloned.1.call-update) | async-done | bytes 524304 | tf_op jit(solution)/shard_map/reduce_scatter | solution.py:51
  856.0 111.1 %reduce-scatter.6.cloned.1.call-done = f32[2048,64]{0,1:T(8,128)} async-done(((f32[65536,64]{0,1:T(8,128)}), f32[2048,64]{0,1:T(8,128)}) %reduce-scatter.6.cloned.1.call-update) | async-done | bytes 524304 | tf_op jit(solution)/shard_map/reduce_scatter | solution.py:50
  (6 shorter events, 0.0 us)
Async XLA Ops:
  7.2 115.4 %all-gather.3.cloned.1.call-start = ((), (), s32[]{:S(2)}) async-start(), calls=%async_computation.3 | async-start | bytes 34603008 | tf_op jit(solution)/shard_map/all_gather | solution.py:20
  8.0 240.5 %all-gather.5.cloned.1.call-start = ((), (), s32[]{:S(2)}) async-start(), calls=%async_computation.4 | async-start | bytes 34603008 | tf_op jit(solution)/shard_map/all_gather | solution.py:21
  8.8 737.3 %reduce-scatter.4.cloned.1.call-start = ((), (), s32[]{:S(2)}) async-start(), calls=%async_computation.5 | async-start | bytes 69206016 | tf_op jit(solution)/shard_map/reduce_scatter | solution.py:44
  154.0 15.8 %copy-start.4 = (bf16[64,2048,1]{1,0,2:T(8,128)(2,1)}, bf16[64,2048,1]{1,0,2:T(8,128)(2,1)S(1)}, u32[]{:S(2)}) copy-start(bf16[64,2048,1]{1,0,2:T(8,128)(2,1)S(1)} %fusion.36) | copy-start | bytes 786436
  169.8 31.7 %copy-start.6 = (bf16[4,2048,64]{1,2,0:T(8,128)(2,1)}, bf16[4,2048,64]{1,2,0:T(8,128)(2,1)S(1)}, u32[]{:S(2)}) copy-start(bf16[4,2048,64]{1,2,0:T(8,128)(2,1)S(1)} %fusion.30) | copy-start | bytes 3145732
  248.4 32.9 %copy-start = (bf16[4,2048,64]{1,2,0:T(8,128)(2,1)}, bf16[4,2048,64]{1,2,0:T(8,128)(2,1)S(1)}, u32[]{:S(2)}) copy-start(bf16[4,2048,64]{1,2,0:T(8,128)(2,1)S(1)} %convolution_convert_fusion) | copy-start | bytes 3145732
  264.7 16.6 %copy-start.8 = (bf16[4,2048,64]{1,2,0:T(8,128)(2,1)}, bf16[4,2048,64]{1,2,0:T(8,128)(2,1)S(1)}, u32[]{:S(2)}) copy-start(bf16[4,2048,64]{1,2,0:T(8,128)(2,1)S(1)} %get-tuple-element.10) | copy-start | bytes 3145732
  281.3 36.0 %copy-start.7 = (bf16[4,2048,64]{1,2,0:T(8,128)(2,1)S(1)}, bf16[4,2048,64]{1,2,0:T(8,128)(2,1)}, u32[]{:S(2)}) copy-start(bf16[4,2048,64]{1,2,0:T(8,128)(2,1)} %copy-done.6) | copy-start | bytes 3145732
  317.3 16.4 %copy-start.5 = (bf16[64,2048,1]{1,0,2:T(8,128)(2,1)S(1)}, bf16[64,2048,1]{1,0,2:T(8,128)(2,1)}, u32[]{:S(2)}) copy-start(bf16[64,2048,1]{1,0,2:T(8,128)(2,1)} %copy-done.4) | copy-start | bytes 786436
  333.7 38.2 %copy-start.2 = (bf16[2048,64]{0,1:T(8,128)(2,1)}, bf16[2048,64]{0,1:T(8,128)(2,1)S(1)}, u32[]{:S(2)}) copy-start(bf16[2048,64]{0,1:T(8,128)(2,1)S(1)} %fusion.34) | copy-start | bytes 786436
  462.7 393.3 %reduce-scatter.8.cloned.1.call-start = ((), (), s32[]{:S(2)}) async-start(), calls=%async_computation.7 | async-start | bytes 17301504 | tf_op jit(solution)/shard_map/reduce_scatter | solution.py:51
  476.7 25.4 %copy-start.3 = (bf16[2048,64]{0,1:T(8,128)(2,1)S(1)}, bf16[2048,64]{0,1:T(8,128)(2,1)}, u32[]{:S(2)}) copy-start(bf16[2048,64]{0,1:T(8,128)(2,1)} %copy-done.2) | copy-start | bytes 786436
  523.5 20.9 %slice-start = ((s8[16777216]{0:T(1024)(128)(4,1)}), s8[4194304]{0:T(1024)(128)(4,1)S(1)}, s32[]{:S(2)}) async-start(s8[16777216]{0:T(1024)(128)(4,1)} %bitcast.99), calls=%async_computation.8 | async-start | bytes 8388608
  523.5 20.9 %slice-start.1 = ((s8[16777216]{0:T(1024)(128)(4,1)}), s8[4194304]{0:T(1024)(128)(4,1)S(1)}, s32[]{:S(2)}) async-start(s8[16777216]{0:T(1024)(128)(4,1)} %bitcast.99), calls=%async_computation.9 | async-start | bytes 8388608
  523.5 20.9 %slice-start.2 = ((s8[16777216]{0:T(1024)(128)(4,1)}), s8[4194304]{0:T(1024)(128)(4,1)S(1)}, s32[]{:S(2)}) async-start(s8[16777216]{0:T(1024)(128)(4,1)} %bitcast.99), calls=%async_computation.10 | async-start | bytes 8388608
  523.5 20.9 %slice-start.3 = ((s8[16777216]{0:T(1024)(128)(4,1)}), s8[4194304]{0:T(1024)(128)(4,1)S(1)}, s32[]{:S(2)}) async-start(s8[16777216]{0:T(1024)(128)(4,1)} %bitcast.99), calls=%async_computation.11 | async-start | bytes 8388608
  561.0 1.2 copy-start.1
  561.0 406.0 %reduce-scatter.6.cloned.1.call-start = ((), (), s32[]{:S(2)}) async-start(), calls=%async_computation.6 | async-start | bytes 17301504 | tf_op jit(solution)/shard_map/reduce_scatter | solution.py:50
Sparse Core Ops, SparseCore 0:
  10.1 112.4 all-gather.2
  124.7 107.4 all-gather.4
  462.8 283.1 reduce-scatter.3
  750.2 105.7 reduce-scatter.7
  860.2 106.8 reduce-scatter.5
where the time goes:
time: 984 us; the launch traced here: 974 us
  waiting for transfers between devices  480 us (49%)
  matrix products  369 us (38%)
  other arithmetic  56.1 us (6%)
  local copies, waits for them, and re-layouts  54.8 us (6%)
  between operations  14.5 us (1%)
    reduce_scatter x1, waiting for transfers between devices, local_grads(): lax.psum_scatter(dx_part, 'tp', scatter_dimension=0, tiled=True)  150 us
    reduce_scatter x1, waiting for transfers between devices, local_grads(): dwk_blk = lax.psum_scatter(wk_buf, 'tp', scatter_dimension=0, tiled=True)  111 us
    all_gather x1, waiting for transfers between devices, local_grads(): x_full = lax.all_gather(x_blk, 'tp', axis=0, tiled=True)  110 us
    reduce_scatter x1, waiting for transfers between devices, local_grads(): dwv_blk = lax.psum_scatter(wv_buf, 'tp', scatter_dimension=0, tiled=True)  107 us
    dot_general x1, matrix products, local_grads(): jnp.einsum('hte,che->tc', d_query, wq_loc, preferred_element_type=f32)  66.4 us
    unnamed x30, local copies, waits for them, and re-layouts  39.3 us
    dot_general x1, matrix products, local_grads(): jnp.einsum('hqe,ke->hqk', d_out, val_rows, preferred_element_type=f32)  36 us
    convert_element_type x1, other arithmetic, local_grads(): prob_bf = attn_prob.astype(bf16)  32.8 us
  transfers between devices with their start and end apart: 5, of which 4 were waited for; matrix products, arithmetic and copies ran while one was open for 27% of the time, Pallas kernels for 0%

commit v1 on v0

v1 whole, which is shorter than its diff:
```python
import functools
import math

import jax
import jax.numpy as jnp
from jax import lax
from jax.experimental import pallas as pl
from jax.experimental.pallas import tpu as pltpu
from jax.sharding import PartitionSpec as P

F32 = jnp.float32
BF16 = jnp.bfloat16
MESH = pl.DeviceIdType.MESH
ANY = pl.BlockSpec(memory_space=pl.ANY)
VMEM = pl.BlockSpec(memory_space=pltpu.VMEM)
LOG2E = math.log2(math.e)
ORDER = (2, 1, 3, 0)


def _dot(a, b, dims):
    return lax.dot_general(a, b, (dims, ((), ())), preferred_element_type=F32)


def _nn(a, b):
    return _dot(a, b, ((1,), (0,)))


def _nt(a, b):
    return _dot(a, b, ((1,), (1,)))


class Place:
    def __init__(self, ring, cores):
        me = lax.axis_index("tp")
        self.ring, self.cores = ring, cores
        self.c = lax.rem(me, cores)
        self.x = lax.rem(me // cores, ring)
        self.y = me // (cores * ring)
        self.r = self.x * cores + self.c
        self.n_row = ring * cores

    def dev(self, y, x, c):
        y = lax.rem(y + self.ring, self.ring)
        x = lax.rem(x + self.ring, self.ring)
        return {"tp": (y * self.ring + x) * self.cores + c}

    def row_dev(self, r):
        return {"tp": self.y * self.n_row + r}

    def slot(self, x, c):
        return lax.rem(x + self.ring, self.ring) * self.cores + c


def _remote(src, dst, send, recv, dev):
    return pltpu.make_async_remote_copy(
        src_ref=src, dst_ref=dst, send_sem=send, recv_sem=recv, device_id=dev, device_id_type=MESH
    )


def _enter(devices):
    barrier = pltpu.get_barrier_semaphore()
    for dev in devices:
        pl.semaphore_signal(barrier, inc=1, device_id=dev, device_id_type=MESH)
    pl.semaphore_wait(barrier, len(devices))


def _proj_kernel(w_ref, x_ref, o_ref):
    o_ref[...] = _nt(w_ref[...], x_ref[...]).astype(BF16)


def _proj(w, x, block):
    n, width = w.shape
    tokens = x.shape[0]
    return pl.pallas_call(
        _proj_kernel,
        name="proj",
        grid=(tokens // block,),
        in_specs=[pl.BlockSpec((n, width), lambda i: (0, 0)), pl.BlockSpec((block, width), lambda i: (i, 0))],
        out_specs=pl.BlockSpec((n, block), lambda i: (0, i)),
        out_shape=jax.ShapeDtypeStruct((n, tokens), BF16),
        compiler_params=pltpu.CompilerParams(vmem_limit_bytes=48 << 20),
        cost_estimate=pl.CostEstimate(flops=2 * n * width * tokens, bytes_accessed=2 * (n + tokens) * width, transcendentals=0),
    )(w, x)


def _attn_kernel(ring, cores, heads, scale, bq, qkvt_ref, dot_ref, wq_ref, g_ref, dqt_ref, ot_ref, wrow_ref,
                 s_ref, dk_ref, dv_ref, w_buf, send, recv, local):
    at = Place(ring, cores)
    n_row = at.n_row
    e = qkvt_ref.shape[0] // (heads + 2)
    tokens = qkvt_ref.shape[1]
    cw = wrow_ref.shape[2]
    peers = [lax.rem(at.r + d, n_row) for d in range(n_row)]
    _enter([at.row_dev(r) for r in peers[1:]])
    copies = []
    for d in range(1, n_row):
        cols = pl.ds(pl.multiple_of(peers[d] * cw, cw), cw)
        cp = _remote(wq_ref.at[:, cols], wrow_ref.at[at.r], send.at[d], recv.at[d], at.row_dev(peers[d]))
        cp.start()
        copies.append(cp)
    own_in = pltpu.make_async_copy(wq_ref.at[:, pl.ds(pl.multiple_of(at.r * cw, cw), cw)], w_buf, local.at[0])
    own_in.start()
    own_in.wait()
    own_out = pltpu.make_async_copy(w_buf, wrow_ref.at[at.r], local.at[1])
    own_out.start()

    dk_ref[...] = jnp.zeros_like(dk_ref)
    dv_ref[...] = jnp.zeros_like(dv_ref)
    krow, vrow = heads * e, (heads + 1) * e
    row = lax.broadcasted_iota(jnp.int32, (bq, bq), 0)
    col = lax.broadcasted_iota(jnp.int32, (bq, bq), 1)
    for i in range(tokens // bq):
        q0 = i * bq
        chunks = [slice(k, k + bq) for k in range(0, q0 + bq, bq)]
        qs = slice(q0, q0 + bq)

        def head(h, _, q0=q0, chunks=chunks, qs=qs):
            hs = pl.ds(pl.multiple_of(h * e, e), e)
            qt = qkvt_ref[hs, qs]
            dot = dot_ref[hs, qs]
            q = qt.T
            do = dot.T
            m = None
            for ks in chunks:
                s = _nn(q, qkvt_ref[krow:krow + e, ks])
                if ks.start == q0:
                    s = jnp.where(row >= col, s, -jnp.inf)
                s_ref[:, ks] = s
                part = s[:, :128]
                for t in range(128, bq, 128):
                    part = jnp.maximum(part, s[:, t:t + 128])
                m = part if m is None else jnp.maximum(m, part)
            m = jnp.max(m, axis=1, keepdims=True)
            total = None
            for ks in chunks:
                p = jnp.exp2((s_ref[:, ks] - m) * (scale * LOG2E))
                s_ref[:, ks] = p
                part = p[:, :128]
                for t in range(128, bq, 128):
                    part = part + p[:, t:t + 128]
                total = part if total is None else total + part
            inv = 1.0 / jnp.sum(total, axis=1, keepdims=True)
            out = None
            for ks in chunks:
                p = s_ref[:, ks] * inv
                s_ref[:, ks] = p
                pb = p.astype(BF16)
                part = _nt(pb, qkvt_ref[vrow:vrow + e, ks])
                out = part if out is None else out + part
                dv_ref[:, ks] += _nn(dot, pb)
            out = out.astype(BF16)
            ot_ref[hs, qs] = out.T
            delta = jnp.sum(do.astype(F32) * out.astype(F32), axis=1, keepdims=True)
            dq = None
            for ks in chunks:
                dp = _nn(do, qkvt_ref[vrow:vrow + e, ks])
                ds = (s_ref[:, ks] * (dp - delta)).astype(BF16)
                part = _nt(ds, qkvt_ref[krow:krow + e, ks])
                dq = part if dq is None else dq + part
                dk_ref[:, ks] += _nn(qt, ds)
            dqt_ref[hs, qs] = (dq * scale).astype(BF16).T
            return 0

        lax.fori_loop(0, heads, head, 0)
        g_ref[qs, 0:heads * e] = dqt_ref[:, qs].T
    for k in range(0, tokens, bq):
        ks = slice(k, k + bq)
        g_ref[ks, heads * e:(heads + 1) * e] = (dk_ref[:, ks] * scale).astype(BF16).T
        g_ref[ks, (heads + 1) * e:(heads + 2) * e] = dv_ref[:, ks].astype(BF16).T
    own_out.wait()
    for cp in copies:
        cp.wait()


def _attention(ring, cores, heads, scale, qkvt, dot, wq):
    tokens = qkvt.shape[1]
    e = qkvt.shape[0] // (heads + 2)
    n_row = ring * cores
    cw = wq.shape[1] // n_row
    bq = min(256, tokens)
    return pl.pallas_call(
        functools.partial(_attn_kernel, ring, cores, heads, scale, bq),
        name="attn",
        in_specs=[VMEM, VMEM, ANY],
        out_specs=[VMEM, VMEM, VMEM, ANY],
        out_shape=[
            jax.ShapeDtypeStruct((tokens, (heads + 2) * e), BF16),
            jax.ShapeDtypeStruct((heads * e, tokens), BF16),
            jax.ShapeDtypeStruct((heads * e, tokens), BF16),
            jax.ShapeDtypeStruct((n_row, heads * e, cw), BF16),
        ],
        scratch_shapes=[
            pltpu.VMEM((bq, tokens), F32),
            pltpu.VMEM((e, tokens), F32),
            pltpu.VMEM((e, tokens), F32),
            pltpu.VMEM((heads * e, cw), BF16),
            pltpu.SemaphoreType.DMA((n_row,)),
            pltpu.SemaphoreType.DMA((n_row,)),
            pltpu.SemaphoreType.DMA((2,)),
        ],
        compiler_params=pltpu.CompilerParams(collective_id=0, has_side_effects=True, vmem_limit_bytes=40 << 20),
        cost_estimate=pl.CostEstimate(flops=12 * heads * tokens * tokens * e, bytes_accessed=8 << 20, transcendentals=heads * tokens * tokens // 2),
    )(qkvt, dot, wq)


def _grads_kernel(ring, cores, heads, g_ref, wrow_ref, wkv_ref, dqt_ref, ot_ref, x_ref, dy_ref,
                  dx_ref, dwq_ref, dwo_ref, dwk_ref, dwv_ref,
                  gq, w_all, part, rs_half, rs_full, stage, xbuf, obuf, kvt,
                  ag_send, ag_recv, rs_send, rs_recv, out_send, out_recv, in_sem, o_sem, ld_sem):
    at = Place(ring, cores)
    n_row = at.n_row
    tokens, width = x_ref.shape
    gw = g_ref.shape[1]
    hd = dqt_ref.shape[0]
    e = hd // heads
    tb = tokens // ring
    th = tb // 2
    tl = tb // n_row
    cw = w_all.shape[1]
    hw = cw // 2
    half_a, half_b = pl.ds(0, hw), pl.ds(hw, hw)
    n_ld = 2 * n_row + 1

    def gcols(slot):
        return pl.ds(pl.multiple_of(slot * gw, gw), gw)

    loads = [pltpu.make_async_copy(g_ref, gq.at[:, gcols(at.r)], ld_sem.at[0])]
    per_kv = n_row // wkv_ref.shape[0]
    for r in range(n_row):
        loads.append(pltpu.make_async_copy(wrow_ref.at[r], w_all.at[pl.ds(r * gw, hd), :], ld_sem.at[1 + r]))
        loads.append(pltpu.make_async_copy(wkv_ref.at[r // per_kv], w_all.at[pl.ds(r * gw + hd, gw - hd), :], ld_sem.at[1 + n_row + r]))
    for cp in loads:
        cp.start()

    up, down = at.dev(at.y + 1, at.x, at.c), at.dev(at.y - 1, at.x, at.c)
    right, left = at.dev(at.y, at.x + 1, at.c), at.dev(at.y, at.x - 1, at.c)
    mate = at.dev(at.y, at.x, 1 - at.c)
    peers = [lax.rem(at.r + d, n_row) for d in range(n_row)]
    _enter([up, down] + [at.row_dev(r) for r in peers[1:]])
    loads[0].wait()

    s_own, s_left, s_right, s_far = at.r, at.slot(at.x - 1, at.c), at.slot(at.x + 1, at.c), at.slot(at.x + 2, at.c)
    m_own, m_left, m_right, m_far = at.slot(at.x, 1 - at.c), at.slot(at.x - 1, 1 - at.c), at.slot(at.x + 1, 1 - at.c), at.slot(at.x + 2, 1 - at.c)
    blocks = [lax.rem(at.y + o, ring) for o in ORDER]
    sends = []

    def piece(k, slot, half=None):
        r0 = pl.multiple_of(blocks[k] * tb, tb)
        rows = pl.ds(r0, tb) if half is None else pl.ds(pl.multiple_of(r0 + half * th, th), th)
        return gq.at[rows, gcols(slot)]

    def ag_send_piece(k, n, slot, dev, half=None):
        ref = piece(k, slot, half)
        cp = _remote(ref, ref, ag_send.at[k, n], ag_recv.at[k, n], dev)
        cp.start()
        sends.append(cp)

    def ag_wait(k, n, slot, half=None):
        ref = piece(k, slot, half)
        _remote(ref, ref, ag_send.at[k, n], ag_recv.at[k, n], mate).wait_recv()

    def ag_own(k):
        ag_send_piece(k, 0, s_own, right)
        ag_send_piece(k, 1, s_own, left)
        ag_send_piece(k, 2, s_own, mate)

    def ag_relay(k):
        ag_wait(k, 0, s_left)
        ag_send_piece(k, 3, s_left, right, 0)
        ag_send_piece(k, 4, s_left, mate)
        ag_wait(k, 1, s_right)
        ag_send_piece(k, 5, s_right, left, 1)
        ag_send_piece(k, 6, s_right, mate)

    def ag_finish(k):
        ag_wait(k, 3, s_far, 0)
        ag_send_piece(k, 7, s_far, mate, 0)
        ag_wait(k, 5, s_far, 1)
        ag_send_piece(k, 8, s_far, mate, 1)
        ag_wait(k, 2, m_own)
        ag_wait(k, 4, m_left)
        ag_wait(k, 6, m_right)
        ag_wait(k, 7, m_far, 0)
        ag_wait(k, 8, m_far, 1)

    nt = min(256, cw)

    def partial(k):
        rows = pl.ds(pl.multiple_of(blocks[k] * tb, tb), tb)

        def tile(j, _):
            cs = pl.ds(pl.multiple_of(j * nt, nt), nt)
            part[k, :, cs] = _nn(gq[rows, :], w_all[:, cs])
            return 0

        lax.fori_loop(0, cw // nt, tile, 0)

    def rs_send_piece(n, src, dst, dev):
        cp = _remote(src, dst, rs_send.at[n], rs_recv.at[n], dev)
        cp.start()
        sends.append(cp)

    def rs_wait(n, ref):
        _remote(ref, ref, rs_send.at[n], rs_recv.at[n], mate).wait_recv()

    bc = xbuf.shape[2]
    n_steps = width // bc

    def stream(src, lhs, out, j0, j1):
        def load(j, slot):
            return pltpu.make_async_copy(src.at[:, pl.ds(pl.multiple_of(j * bc, bc), bc)], xbuf.at[slot], in_sem.at[slot])

        def store(j, slot):
            return pltpu.make_async_copy(obuf.at[slot], out.at[:, pl.ds(pl.multiple_of(j * bc, bc), bc)], o_sem.at[slot])

        if j0 == 0:
            load(0, 0).start()

        def step(j, _):
            slot = lax.rem(j, 2)

            @pl.when(j + 1 < n_steps)
            def _():
                load(j + 1, 1 - slot).start()

            load(j, slot).wait()

            @pl.when(j >= 2)
            def _():
                store(j - 2, slot).wait()

            obuf[slot] = _nn(lhs[...], xbuf[slot])
            store(j, slot).start()
            return 0

        lax.fori_loop(j0, j1, step, 0)
        if j1 == n_steps:
            for j in range(max(n_steps - 2, 0), n_steps):
                store(j, j % 2).wait()

    cut = [n_steps * q // 4 for q in range(5)]

    ag_own(0)
    stream(dy_ref, ot_ref, dwo_ref, cut[0], cut[2])
    ag_relay(0)
    ag_own(1)
    stream(dy_ref, ot_ref, dwo_ref, cut[2], cut[3])
    ag_finish(0)
    for cp in loads[1:]:
        cp.wait()
    partial(0)
    rs_send_piece(0, part.at[0, :, half_a], rs_half.at[0], up)
    rs_send_piece(1, part.at[0, :, half_b], rs_half.at[1], down)
    stream(dy_ref, ot_ref, dwo_ref, cut[3], cut[4])
    ag_relay(1)
    ag_own(2)
    stream(x_ref, dqt_ref, dwq_ref, cut[0], cut[1])
    ag_finish(1)
    partial(1)
    rs_send_piece(2, part.at[1, :, half_b], rs_full.at[0, :, half_b], up)
    ag_relay(2)
    ag_own(3)
    stream(x_ref, dqt_ref, dwq_ref, cut[1], cut[2])
    ag_finish(2)
    partial(2)
    rs_send_piece(4, part.at[2, :, half_a], rs_full.at[1, :, half_a], down)
    ag_relay(3)
    rs_wait(0, rs_half.at[0])
    part[1, :, half_a] += rs_half[0]
    rs_wait(1, rs_half.at[1])
    part[2, :, half_b] += rs_half[1]
    rs_send_piece(3, part.at[1, :, half_a], rs_full.at[0, :, half_a], up)
    rs_send_piece(5, part.at[2, :, half_b], rs_full.at[1, :, half_b], down)
    ag_finish(3)
    partial(3)
    stream(x_ref, dqt_ref, dwq_ref, cut[2], cut[4])

    n_kv = wkv_ref.shape[0]
    first = (at.r // per_kv) * per_kv
    for q in range(per_kv):
        cols = pl.ds(pl.multiple_of((first + q) * gw + hd, 128), gw - hd)
        for t in range(0, tokens, th):
            kvt[q * (gw - hd):(q + 1) * (gw - hd), t:t + th] = gq[t:t + th, cols].T
    share = width // per_kv
    col0 = lax.rem(at.r, per_kv) * share

    def kv_load(j, slot):
        cs = pl.ds(pl.multiple_of(col0 + j * bc, bc), bc)
        return pltpu.make_async_copy(x_ref.at[:, cs], xbuf.at[slot], in_sem.at[slot])

    def kv_step(j, _):
        slot = lax.rem(j, 2)

        @pl.when(j + 1 < share // bc)
        def _():
            kv_load(j + 1, 1 - slot).start()

        kv_load(j, slot).wait()
        prod = _nn(kvt[...], xbuf[slot])
        dk = dv = None
        for q in range(per_kv):
            a = prod[q * 2 * e:q * 2 * e + e]
            b = prod[q * 2 * e + e:(q + 1) * 2 * e]
            dk = a if dk is None else dk + a
            dv = b if dv is None else dv + b
        cs = pl.ds(pl.multiple_of(j * bc, bc), bc)
        dwk_ref[:, cs] = dk
        dwv_ref[:, cs] = dv
        return 0

    kv_load(0, 0).start()
    lax.fori_loop(0, share // bc, kv_step, 0)

    rs_wait(4, rs_full.at[1, :, half_a])
    rs_wait(3, rs_full.at[0, :, half_a])
    rs_wait(2, rs_full.at[0, :, half_b])
    rs_wait(5, rs_full.at[1, :, half_b])
    stage[...] = (part[3] + rs_full[0] + rs_full[1]).astype(BF16)
    my_cols = pl.ds(pl.multiple_of(at.r * cw, cw), cw)
    for d in range(1, n_row):
        rows = pl.ds(pl.multiple_of(peers[d] * tl, tl), tl)
        cp = _remote(stage.at[rows, :], dx_ref.at[:, my_cols], out_send.at[d], out_recv.at[d], at.row_dev(peers[d]))
        cp.start()
        sends.append(cp)
    keep = pltpu.make_async_copy(stage.at[pl.ds(pl.multiple_of(at.r * tl, tl), tl), :], dx_ref.at[:, my_cols], ld_sem.at[0])
    keep.start()
    for d in range(1, n_row):
        src = lax.rem(at.r + n_row - d, n_row)
        ref = dx_ref.at[:, pl.ds(pl.multiple_of(src * cw, cw), cw)]
        _remote(ref, ref, out_send.at[d], out_recv.at[d], mate).wait_recv()
    keep.wait()
    for cp in sends:
        cp.wait_send()


def _grads(ring, cores, heads, g, wrow, wkv, dqt, ot, x, dy):
    tokens, width = x.shape
    n_row = ring * cores
    hd = dqt.shape[0]
    e = hd // heads
    gw = g.shape[1]
    tb = tokens // ring
    cw = width // n_row
    per_kv = n_row // wkv.shape[0]
    bc = min(512, cw // 2)
    dma = pltpu.SemaphoreType.DMA
    return pl.pallas_call(
        functools.partial(_grads_kernel, ring, cores, heads),
        name="grads",
        in_specs=[ANY, ANY, ANY, VMEM, VMEM, ANY, ANY],
        out_specs=[ANY, ANY, ANY, VMEM, VMEM],
        out_shape=[
            jax.ShapeDtypeStruct((tb // n_row, width), BF16),
            jax.ShapeDtypeStruct((hd, width), F32),
            jax.ShapeDtypeStruct((hd, width), F32),
            jax.ShapeDtypeStruct((e, width // per_kv), F32),
            jax.ShapeDtypeStruct((e, width // per_kv), F32),
        ],
        scratch_shapes=[
            pltpu.VMEM((tokens, n_row * gw), BF16),
            pltpu.VMEM((n_row * gw, cw), BF16),
            pltpu.VMEM((ring, tb, cw), F32),
            pltpu.VMEM((2, tb, cw // 2), F32),
            pltpu.VMEM((2, tb, cw), F32),
            pltpu.VMEM((tb, cw), BF16),
            pltpu.VMEM((2, tokens, bc), BF16),
            pltpu.VMEM((2, hd, bc), F32),
            pltpu.VMEM((per_kv * (gw - hd), tokens), BF16),
            dma((ring, 9)),
            dma((ring, 9)),
            dma((6,)),
            dma((6,)),
            dma((n_row,)),
            dma((n_row,)),
            dma((2,)),
            dma((2,)),
            dma((2 * n_row + 1,)),
        ],
        compiler_params=pltpu.CompilerParams(collective_id=1, has_side_effects=True, vmem_limit_bytes=60 << 20),
        cost_estimate=pl.CostEstimate(flops=2 * tokens * width * (n_row * gw // n_row + 3 * hd), bytes_accessed=100 << 20, transcendentals=0),
    )(g, wrow, wkv, dqt, ot, x, dy)


def solution(mesh):
    n = mesh.shape["tp"]
    ring = math.isqrt(n // 2)
    cores = n // (ring * ring)
    if ring != 4 or cores != 2:
        raise ValueError("needs a 4x4 torus")

    def local_grads(x_blk, dy_blk, wq_loc, w_k, w_v, wo_loc):
        model_dim, kv_heads, e = w_k.shape
        heads = wq_loc.shape[1]
        hd = heads * e
        n_row = ring * cores
        scale = e ** -0.5
        me = lax.axis_index("tp")
        wq = jnp.transpose(wq_loc, (1, 2, 0)).reshape(hd, model_dim)
        wk = jnp.transpose(w_k, (1, 2, 0))
        wv = jnp.transpose(w_v, (1, 2, 0))
        wo = wo_loc.reshape(hd, model_dim)
        j = me // (n // kv_heads)
        w_in = jnp.concatenate([wq, lax.dynamic_index_in_dim(wk, j, 0, False), lax.dynamic_index_in_dim(wv, j, 0, False)])
        kv_row = kv_heads // ring
        cw = model_dim // n_row
        start = ((me // n_row) * kv_row, 0, lax.rem(me, n_row) * cw)
        wkv = jnp.concatenate([lax.dynamic_slice(w, start, (kv_row, e, cw)) for w in (wk, wv)], axis=1)

        x_full = lax.all_gather(x_blk, "tp", axis=0, tiled=True)
        dy_full = lax.all_gather(dy_blk, "tp", axis=0, tiled=True)
        tokens = x_full.shape[0]
        block = min(512, tokens)
        qkvt = _proj(w_in, x_full, block)
        dot = _proj(wo, dy_full, block)
        g, dqt, ot, wrow = _attention(ring, cores, heads, scale, qkvt, dot, wq)
        dx, dwq, dwo, dwk, dwv = _grads(ring, cores, heads, g, wrow, wkv, dqt, ot, x_full, dy_full)
        return (dx, jnp.transpose(dwq.reshape(heads, e, model_dim), (2, 0, 1)), dwo.reshape(heads, e, model_dim), dwk.T, dwv.T)

    tok = P(("dp", "tp"))
    return jax.shard_map(
        local_grads,
        mesh=mesh,
        in_specs=(tok, tok, P(None, "tp", None), P(), P(), P("tp")),
        out_specs=(tok, P("dp", "tp", None), tok, tok, tok),
        check_vma=False,
    )
```

time: 984 us -> 472 us (0.48)
  matrix products: 369 us -> 0 us
  waiting for transfers between devices: 480 us -> 199 us
  Pallas kernels: 0 us -> 226 us
  other arithmetic: 56.1 us -> 6.6 us
  local copies, waits for them, and re-layouts: 54.8 us -> 25.5 us
    reduce_scatter x3 -> x0, waiting for transfers between devices: 368 us -> none  [the longest x1 150 us: local_grads(): lax.psum_scatter(dx_part, 'tp', scatter_dimension=0, tiled=True)]
    dot_general x16 -> x0, matrix products: 337 us -> none  [the longest x1 66.4 us: local_grads(): jnp.einsum('hte,che->tc', d_query, wq_loc, preferred_element_type=f32)]
    pallas_call x0 -> x4, Pallas kernels: none -> 226 us  [the longest x1 122 us: _grads(): pl.pallas_call(functools.partial(_grads_kernel, ring, cores, heads), name...]
    all_gather x1, waiting for transfers between devices: 0.02 us -> 104 us  [local_grads(): dy_full = lax.all_gather(dy_blk, 'tp', axis=0, tiled=True)]
    convert_element_type x2 -> x0, other arithmetic: 35.4 us -> none  [the longest x1 32.8 us: local_grads(): prob_bf = attn_prob.astype(bf16)]
    sub x1 -> x0, matrix products: 31.6 us -> none  [local_grads(): attn_prob = jax.nn.softmax(scores, axis=-1)]
    unnamed x30 -> x25, local copies, waits for them, and re-layouts: 39.3 us -> 22.5 us
    select_n x1 -> x0, other arithmetic: 16.5 us -> none  [local_grads(): jnp.where(slot, wv_part[None], 0.0).reshape(kv_heads * model_dim, head_dim)]
  transfers between devices with their start and end apart: 5 -> 2, of which waited for: 4 -> 2; matrix products, arithmetic and copies ran while one was open for 27% -> 2% of each run, Pallas kernels for 0% -> 3%
where the time goes in v1:
time: 472 us; the launch traced here: 471 us
  Pallas kernels  226 us (48%)
  waiting for transfers between devices  199 us (42%)
  local copies, waits for them, and re-layouts  25.5 us (5%)
  between operations  14.2 us (3%)
  other arithmetic  6.6 us (1%)
    pallas_call x1, Pallas kernels, _grads(): pl.pallas_call(functools.partial(_grads_kernel, ring, cores, heads), name...  122 us
    all_gather x1, waiting for transfers between devices, local_grads(): dy_full = lax.all_gather(dy_blk, 'tp', axis=0, tiled=True)  104 us
    all_gather x1, waiting for transfers between devices, local_grads(): x_full = lax.all_gather(x_blk, 'tp', axis=0, tiled=True)  93.2 us
    pallas_call x1, Pallas kernels, _attention(): pl.pallas_call(functools.partial(_attn_kernel, ring, cores, heads, scale,...  70.6 us
    pallas_call x2, Pallas kernels, _proj(): pl.pallas_call(_proj_kernel, name='proj', grid=(tokens // block,), in_spe...  33.2 us
    unnamed x25, local copies, waits for them, and re-layouts  22.5 us
  transfers between devices with their start and end apart: 2, of which 2 were waited for; matrix products, arithmetic and copies ran while one was open for 2% of the time, Pallas kernels for 3%

profile of v1, /device:TPU:97, one launch (start us, length us, event | category | flops | bytes accessed | tf_op | source)
XLA Modules:
  0.0 470.9 jit_solution(8031992367280612873)
XLA Ops:
  7.2 0.1 all-gather.5.cloned.1.call-start
  7.2 0.7 all-gather.5.cloned.1.call-update
  8.0 0.1 all-gather.3.cloned.1.call-start
  8.0 0.7 all-gather.3.cloned.1.call-update
  8.8 0.0 copy-start.5
  8.8 1.2 dynamic-slice_bitcast_fusion.2
  10.1 0.8 pad_maximum_fusion.1.wkv_ref
  10.9 1.7 dynamic-slice_bitcast_fusion
  12.6 0.0 copy-done.5
  12.6 5.8 %pad_maximum_fusion.w_ref = bf16[384,8192]{1,0:T(8,128)(2,1)} fusion(bf16[64,8192]{1,0:T(8,128)(2,1)S(1)} %get-tuple-element.23, bf16[64,8192]{1,0:T(8,128)(2,1)S(1)} %get-tuple-element.24, bf16[256,8192]{1,0:T(8,128)(2,1)S(1)} %bitcast.28), kind=kLoop, calls=%fused_computation | loop fusion | flops 18874368 | bytes 12582912 | tf_op jit(solution)/shard_map/concatenate | solution.py:503
  18.4 104.2 %all-gather.5.cloned.1.call-done.x_ref.dy_ref = bf16[2048,8192]{1,0:T(8,128)(2,1)} async-done(((bf16[64,8192]{1,0:T(8,128)(2,1)}), bf16[2048,8192]{1,0:T(8,128)(2,1)}) %all-gather.5.cloned.1.call-update) | async-done | bytes 33554448 | tf_op jit(solution)/shard_map/all_gather | solution.py:510
  122.6 0.0 copy-start
  122.6 2.2 copy-done
  124.8 14.2 %proj.3.dot_ref = bf16[256,2048]{1,0:T(8,128)(2,1)S(1)} custom-call(bf16[256,8192]{1,0:T(8,128)(2,1)S(1)} %bitcast.22, bf16[2048,8192]{1,0:T(8,128)(2,1)} %all-gather.5.cloned.1.call-done.x_ref.dy_ref), custom_call_target="tpu_custom_call" | custom-call | flops 8589934592 | bytes 37748736 | tf_op jit(solution)/shard_map/proj/pallas_call | solution.py:74
  139.0 93.2 %all-gather.3.cloned.1.call-done.x_ref = bf16[2048,8192]{1,0:T(8,128)(2,1)} async-done(((bf16[64,8192]{1,0:T(8,128)(2,1)}), bf16[2048,8192]{1,0:T(8,128)(2,1)}) %all-gather.3.cloned.1.call-update) | async-done | bytes 33554448 | tf_op jit(solution)/shard_map/all_gather | solution.py:509
  232.2 19.0 %proj.2.qkvt_ref = bf16[384,2048]{1,0:T(8,128)(2,1)S(1)} custom-call(bf16[384,8192]{1,0:T(8,128)(2,1)} %pad_maximum_fusion.w_ref, bf16[2048,8192]{1,0:T(8,128)(2,1)} %all-gather.3.cloned.1.call-done.x_ref), custom_call_target="tpu_custom_call" | custom-call | flops 12884901888 | bytes 39845888 | tf_op jit(solution)/shard_map/proj/pallas_call | solution.py:74
  251.2 70.6 %attn.1 = (bf16[2048,384]{1,0:T(8,128)(2,1)S(1)}, bf16[256,2048]{1,0:T(8,128)(2,1)S(1)}, bf16[256,2048]{1,0:T(8,128)(2,1)S(1)}, bf16[8,256,1024]{2,1,0:T(8,128)(2,1)S(1)}) custom-call(bf16[384,2048]{1,0:T(8,128)(2,1)S(1)} %proj.2.qkvt_ref, bf16[256,2048]{1,0:T(8,128)(2,1)S(1)} %proj.3.dot_ref, bf16[256,8192]{1,0:T(8,128)(2,1)} %bitcast.27), custom_call_target="tpu_custom_call" | custom-call | flops 12884901888 | bytes 8388608 | tf_op jit(solution)/shard_map/attn/pallas_call | solution.py:181
  321.9 0.0 copy-start.1
  321.9 2.0 copy-done.1
  323.9 0.0 copy-start.2
  323.9 1.1 copy-done.2
  325.0 0.0 copy-start.3
  325.0 1.0 copy-done.3
  326.0 0.0 copy-start.4
  326.0 1.0 copy-done.4
  327.0 121.8 %grads.1 = (bf16[64,8192]{1,0:T(8,128)(2,1)}, f32[256,8192]{1,0:T(8,128)}, f32[256,8192]{1,0:T(8,128)}, f32[64,2048]{1,0:T(8,128)}, f32[64,2048]{1,0:T(8,128)}) custom-call(bf16[2048,384]{1,0:T(8,128)(2,1)} %copy-done.2, bf16[8,256,1024]{2,1,0:T(8,128)(2,1)} %copy-done.1, bf16[2,128,1024]{2,1,0:T(8,128)(2,1)} %pad_maximum_fusion.1.wkv_ref, ...), custom_call_target="tpu_custom_call" | custom-call | flops 38654705664 | bytes 104857600 | tf_op jit(solution)/shard_map/grads/pallas_call | solution.py:447
  448.8 0.0 slice-start
  448.8 2.4 copy.16
  451.2 0.0 slice-start.1
  451.2 7.8 %copy.17 = f32[8192,4,64]{0,2,1:T(8,128)} copy(f32[8192,4,64]{0,2,1:T(8,128)} %bitcast.26) | data formatting | bytes 16777216
  459.0 0.0 slice-done
  459.0 0.0 slice-done.1
  459.0 0.0 copy-start.7
  459.0 0.0 copy-start.6
  459.1 3.4 copy.18
  462.4 0.0 copy-done.7
  462.5 0.8 copy.19
  463.2 0.0 copy-done.6
  463.2 0.8 copy.20
  (1 shorter events, 0.0 us)
Async XLA Ops:
  7.2 115.4 %all-gather.5.cloned.1.call-start = ((), (), s32[]{:S(2)}) async-start(), calls=%async_computation.1 | async-start | bytes 34603008 | tf_op jit(solution)/shard_map/all_gather | solution.py:510
  8.0 224.2 %all-gather.3.cloned.1.call-start = ((), (), s32[]{:S(2)}) async-start(), calls=%async_computation | async-start | bytes 34603008 | tf_op jit(solution)/shard_map/all_gather | solution.py:509
  8.8 3.8 copy-start.5
  122.6 2.2 copy-start
  321.9 2.0 copy-start.1
  323.9 1.1 copy-start.2
  325.0 1.0 copy-start.3
  326.0 1.0 copy-start.4
  448.8 10.3 %slice-start = ((s8[8388608]{0:T(1024)(128)(4,1)}), s8[4194304]{0:T(1024)(128)(4,1)S(1)}, s32[]{:S(2)}) async-start(s8[8388608]{0:T(1024)(128)(4,1)} %bitcast.23), calls=%async_computation.2 | async-start | bytes 8388608
  451.2 7.8 %slice-start.1 = ((s8[8388608]{0:T(1024)(128)(4,1)}), s8[4194304]{0:T(1024)(128)(4,1)S(1)}, s32[]{:S(2)}) async-start(s8[8388608]{0:T(1024)(128)(4,1)} %bitcast.23), calls=%async_computation.3 | async-start | bytes 8388608
  459.0 3.4 copy-start.7
  459.0 4.2 copy-start.6
Sparse Core Ops, SparseCore 0:
  10.1 112.4 all-gather.4
  124.7 107.4 all-gather.2

commit v2 on v1

--- a/solution.py
+++ b/solution.py
@@ -64,57 +64,225 @@
     pl.semaphore_wait(barrier, len(devices))
 
 
-def _proj_kernel(w_ref, x_ref, o_ref):
-    o_ref[...] = _nt(w_ref[...], x_ref[...]).astype(BF16)
-
-
-def _proj(w, x, block):
-    n, width = w.shape
-    tokens = x.shape[0]
-    return pl.pallas_call(
-        _proj_kernel,
-        name="proj",
-        grid=(tokens // block,),
-        in_specs=[pl.BlockSpec((n, width), lambda i: (0, 0)), pl.BlockSpec((block, width), lambda i: (i, 0))],
-        out_specs=pl.BlockSpec((n, block), lambda i: (0, i)),
-        out_shape=jax.ShapeDtypeStruct((n, tokens), BF16),
-        compiler_params=pltpu.CompilerParams(vmem_limit_bytes=48 << 20),
-        cost_estimate=pl.CostEstimate(flops=2 * n * width * tokens, bytes_accessed=2 * (n + tokens) * width, transcendentals=0),
-    )(w, x)
-
-
-def _attn_kernel(ring, cores, heads, scale, bq, qkvt_ref, dot_ref, wq_ref, g_ref, dqt_ref, ot_ref, wrow_ref,
-                 s_ref, dk_ref, dv_ref, w_buf, send, recv, local):
+OWN, MINUS, PLUS, FAR = range(4)
+STEP = (0, -1, 1, 2)
+
+
+class Gather:
+    def __init__(self, at, src, full, send, recv, mate_recv):
+        self.at, self.src, self.full = at, src, full
+        self.send, self.recv, self.mate_recv = send, recv, mate_recv
+        self.rows = src.shape[0]
+        self.next_send = 0
+        self.sent = []
+        c = at.c
+        self.first = {s: at.dev(at.y + c * s, at.x + (1 - c) * s, c) for s in (1, -1)}
+        self.second = {s: at.dev(at.y + (1 - c) * s, at.x + c * s, c) for s in (1, -1)}
+        self.mate = at.dev(at.y, at.x, 1 - c)
+
+    def ref(self, d1, d2, core, half=None):
+        at = self.at
+        o1, o2 = STEP[d1], STEP[d2]
+        x = at.x + (1 - core) * o1 + core * o2
+        y = at.y + core * o1 + (1 - core) * o2
+        n = self.rows if half is None else self.rows // 2
+        r0 = at.dev(y, x, core)["tp"] * self.rows + (0 if half is None else half * n)
+        return self.full.at[pl.ds(pl.multiple_of(r0, n), n), :]
+
+    def push(self, src, dst, recv, dev):
+        k = self.next_send
+        self.next_send += 1
+        self.sent.append(dst.shape[0])
+        return _remote(src, dst, self.send.at[k], recv, dev)
+
+    def out(self, d1, d2, half=None):
+        if d1 == OWN and d2 == OWN:
+            n = self.rows if half is None else self.rows // 2
+            return self.src.at[pl.ds(0 if half is None else half * n, n), :]
+        return self.ref(d1, d2, self.at.c, half)
+
+    def to_mate(self, d1, d2):
+        ref = self.ref(d1, d2, self.at.c)
+        self.push(self.out(d1, d2), ref, self.mate_recv.at[d1, d2], self.mate).start()
+
+    def arrived(self, d1, d2, half=None):
+        ref = self.ref(d1, d2, self.at.c, half)
+        _remote(ref, ref, self.send.at[0], self.recv.at[d1, d2, half or 0], self.mate).wait_recv()
+
+    def second_full(self, d1):
+        ref = self.ref(d1, OWN, self.at.c)
+        return [self.push(self.out(d1, OWN), ref, self.recv.at[d1, to, 0], self.second[s]) for s, to in ((1, MINUS), (-1, PLUS))]
+
+    def prepare(self):
+        self.fulls = {d: self.second_full(d) for d in range(4)}
+
+    def start(self):
+        ref = self.ref(OWN, OWN, self.at.c)
+        for s, to in ((1, MINUS), (-1, PLUS)):
+            self.push(self.src, ref, self.recv.at[to, OWN, 0], self.first[s]).start()
+        self.go(OWN)
+        self.to_mate(OWN, OWN)
+
+    def go(self, d1):
+        for cp in self.fulls[d1]:
+            cp.start()
+
+    def relay_first(self):
+        for d, s, half in ((MINUS, 1, 0), (PLUS, -1, 1)):
+            self.arrived(d, OWN)
+            ref = self.ref(d, OWN, self.at.c, half)
+            self.push(ref, ref, self.recv.at[FAR, OWN, half], self.first[s]).start()
+            self.to_mate(d, OWN)
+
+    def far_first(self):
+        for half in (0, 1):
+            self.arrived(FAR, OWN, half)
+        self.to_mate(FAR, OWN)
+
+    def relay_second(self, d1):
+        for d, s, half in ((MINUS, 1, 0), (PLUS, -1, 1)):
+            self.arrived(d1, d)
+            ref = self.ref(d1, d, self.at.c, half)
+            self.push(ref, ref, self.recv.at[d1, FAR, half], self.second[s]).start()
+            self.to_mate(d1, d)
+
+    def far_second(self, d1):
+        for half in (0, 1):
+            self.arrived(d1, FAR, half)
+        self.to_mate(d1, FAR)
+
+    def await_mate_row(self, t):
+        at = self.at
+        for j in range(4):
+            i1 = (1 - at.c) * t + at.c * j
+            i2 = at.c * t + (1 - at.c) * j
+            ref = self.full.at[pl.ds(0, self.rows), :]
+            _remote(ref, ref, self.send.at[0], self.mate_recv.at[i1, i2], self.mate).wait_recv()
+
+    def drain(self):
+        for k, n in enumerate(self.sent):
+            ref = self.full.at[pl.ds(0, n), :]
+            _remote(ref, ref, self.send.at[k], self.send.at[k], self.mate).wait_send()
+
+
+def _front_kernel(ring, cores, heads, scale, bq, x_ref, dy_ref, w_ref, wo_ref,
+                  xf_ref, dyf_ref, g_ref, dqt_ref, ot_ref, wrow_ref, hop_ref,
+                  w_v, wo_v, xblk, qkvt_ref, dot_ref, s_ref, dk_ref, dv_ref, w_buf,
+                  send, recv, mate_recv, w_send, w_recv, hop_recv, ld_sem, blk_sem):
     at = Place(ring, cores)
     n_row = at.n_row
-    e = qkvt_ref.shape[0] // (heads + 2)
-    tokens = qkvt_ref.shape[1]
-    cw = wrow_ref.shape[2]
-    peers = [lax.rem(at.r + d, n_row) for d in range(n_row)]
-    _enter([at.row_dev(r) for r in peers[1:]])
-    copies = []
-    for d in range(1, n_row):
-        cols = pl.ds(pl.multiple_of(peers[d] * cw, cw), cw)
-        cp = _remote(wq_ref.at[:, cols], wrow_ref.at[at.r], send.at[d], recv.at[d], at.row_dev(peers[d]))
+    hd = wo_ref.shape[0]
+    e = hd // heads
+    tokens, width = xf_ref.shape
+    tb = tokens // ring
+    cw = width // n_row
+    c = at.c
+    gx = Gather(at, x_ref, xf_ref, send.at[0], recv.at[0], mate_recv.at[0])
+    gy = Gather(at, dy_ref, dyf_ref, send.at[1], recv.at[1], mate_recv.at[1])
+
+    loads = [pltpu.make_async_copy(w_ref, w_v, ld_sem.at[0]), pltpu.make_async_copy(wo_ref, wo_v, ld_sem.at[1])]
+    rows = x_ref.shape[0]
+    own_rows = pl.ds(pl.multiple_of((at.y * n_row + at.r) * rows, rows), rows)
+    ins = [pltpu.make_async_copy(src, xblk.at[i, pl.ds(0, rows), :], ld_sem.at[2 + i]) for i, src in enumerate((x_ref, dy_ref))]
+    outs = [pltpu.make_async_copy(xblk.at[i, pl.ds(0, rows), :], dst.at[own_rows, :], ld_sem.at[4 + i]) for i, dst in enumerate((xf_ref, dyf_ref))]
+    for cp in ins:
         cp.start()
-        copies.append(cp)
-    own_in = pltpu.make_async_copy(wq_ref.at[:, pl.ds(pl.multiple_of(at.r * cw, cw), cw)], w_buf, local.at[0])
-    own_in.start()
-    own_in.wait()
-    own_out = pltpu.make_async_copy(w_buf, wrow_ref.at[at.r], local.at[1])
-    own_out.start()
+    row_peers = [lax.rem(at.r + d, n_row) for d in range(1, n_row)]
+    up, down = at.dev(at.y + 1, at.x, c), at.dev(at.y - 1, at.x, c)
+    _enter([up, down] + [at.row_dev(r) for r in row_peers])
+    gx.prepare()
+    gx.start()
+    for cp in loads:
+        cp.start()
+    for cp in ins:
+        cp.wait()
+    for cp in outs:
+        cp.start()
 
     dk_ref[...] = jnp.zeros_like(dk_ref)
     dv_ref[...] = jnp.zeros_like(dv_ref)
+
+    def project(full, w, out, b):
+        def load(i):
+            r0 = pl.multiple_of(b * tb + i * bq, bq)
+            return pltpu.make_async_copy(full.at[pl.ds(r0, bq), :], xblk.at[i], blk_sem.at[i])
+
+        for i in range(tb // bq):
+            load(i).start()
+
+        def block(i, _):
+            load(i).wait()
+            out[:, pl.ds(pl.multiple_of(b * tb + i * bq, bq), bq)] = _nt(w[...], xblk[i]).astype(BF16)
+            return 0
+
+        lax.fori_loop(0, tb // bq, block, 0)
+
+    def row_at(t):
+        off = jnp.where(t == 1, ring - 1, jnp.where(t == 2, 1, jnp.where(t == 3, 2, 0)))
+        return lax.rem(at.y + off, ring)
+
+    for cp in loads + outs:
+        cp.wait()
+
+    def x_turn(t, _):
+        @pl.when(t == 0)
+        def _():
+            gx.relay_first()
+            gx.go(MINUS)
+
+            @pl.when(c == 0)
+            def _():
+                gx.go(PLUS)
+
+            gx.far_first()
+
+            @pl.when(c == 0)
+            def _():
+                gx.go(FAR)
+
+            gx.relay_second(OWN)
+
+            @pl.when(c == 1)
+            def _():
+                gx.go(PLUS)
+
+            gx.relay_second(MINUS)
+
+            @pl.when(c == 1)
+            def _():
+                gx.go(FAR)
+
+            gx.relay_second(PLUS)
+            gx.far_second(OWN)
+
+        @pl.when(t == 1)
+        def _():
+            gx.relay_second(FAR)
+            gy.start()
+            gx.far_second(MINUS)
+
+        @pl.when(t == 2)
+        def _():
+            gx.far_second(PLUS)
+            gx.far_second(FAR)
+
+        gx.await_mate_row(t)
+        project(xf_ref, w_v, qkvt_ref, row_at(t))
+        return 0
+
+    gy.prepare()
+    lax.fori_loop(0, ring, x_turn, 0)
+
     krow, vrow = heads * e, (heads + 1) * e
     row = lax.broadcasted_iota(jnp.int32, (bq, bq), 0)
     col = lax.broadcasted_iota(jnp.int32, (bq, bq), 1)
-    for i in range(tokens // bq):
+
+    def attend(i):
         q0 = i * bq
         chunks = [slice(k, k + bq) for k in range(0, q0 + bq, bq)]
         qs = slice(q0, q0 + bq)
 
-        def head(h, _, q0=q0, chunks=chunks, qs=qs):
+        def head(h, _):
             hs = pl.ds(pl.multiple_of(h * e, e), e)
             qt = qkvt_ref[hs, qs]
             dot = dot_ref[hs, qs]
@@ -163,44 +331,189 @@
 
         lax.fori_loop(0, heads, head, 0)
         g_ref[qs, 0:heads * e] = dqt_ref[:, qs].T
+
+    hh = hd // 2
+
+    def w_push(k, src, dst, rsem, dev):
+        _remote(src, dst, w_send.at[k], rsem, dev).start()
+
+    def wcols(slot):
+        return pl.ds(pl.multiple_of(slot * cw, cw), cw)
+
+    right, left, mate = at.dev(at.y, at.x + 1, c), at.dev(at.y, at.x - 1, c), at.dev(at.y, at.x, 1 - c)
+
+    def w_start():
+        for half, dev in ((0, right), (1, left)):
+            for k in range(cores):
+                w_push(half * 2 + k, w_ref.at[pl.ds(half * hh, hh), wcols(at.slot(at.x + 2, k))], hop_ref.at[half * 2 + k], hop_recv.at[half * 2 + k], dev)
+        w_push(4, w_ref.at[pl.ds(0, hd), wcols(at.slot(at.x, 1 - c))], wrow_ref.at[at.r], w_recv.at[0], mate)
+        for i, s in enumerate((1, -1)):
+            for k in range(cores):
+                dst_core = c if k == 0 else 1 - c
+                w_push(5 + 2 * i + k, w_ref.at[pl.ds(0, hd), wcols(at.slot(at.x + s, dst_core))], wrow_ref.at[at.r], w_recv.at[1 + 2 * i + k], at.dev(at.y, at.x + s, dst_core))
+
+    def w_relay():
+        for half, s in ((0, 1), (1, -1)):
+            for n in (half * 2, half * 2 + 1):
+                _remote(hop_ref.at[n], hop_ref.at[n], w_send.at[0], hop_recv.at[n], mate).wait_recv()
+            for k in range(cores):
+                n = half * 2 + k
+                src_slot = at.slot(at.x - s, c)
+                same = k == 0
+                dst_core = c if same else 1 - c
+                w_push(9 + n, hop_ref.at[half * 2 + dst_core], wrow_ref.at[src_slot, pl.ds(half * hh, hh), :], w_recv.at[5 + n], at.dev(at.y, at.x + s, dst_core))
+
+    def w_finish():
+        whole = wrow_ref.at[0]
+        part = wrow_ref.at[0, pl.ds(0, hh), :]
+        for n in range(9):
+            ref = whole if n < 5 else part
+            _remote(ref, ref, w_send.at[0], w_recv.at[n], mate).wait_recv()
+        for k in range(13):
+            ref = whole if 4 <= k < 9 else part
+            _remote(ref, ref, w_send.at[k], w_send.at[k], mate).wait_send()
+
+    own_in = pltpu.make_async_copy(w_ref.at[pl.ds(0, hd), wcols(at.r)], w_buf, ld_sem.at[0])
+    own_in.start()
+    own_in.wait()
+    own_out = pltpu.make_async_copy(w_buf, wrow_ref.at[at.r], ld_sem.at[1])
+    own_out.start()
+
+    def turn(t, _):
+        @pl.when(t == 0)
+        def _():
+            gy.relay_first()
+            gy.go(MINUS)
+
+            @pl.when(c == 0)
+            def _():
+                gy.go(PLUS)
+
+            gy.far_first()
+
+            @pl.when(c == 0)
+            def _():
+                gy.go(FAR)
+
+            gy.relay_second(OWN)
+
+            @pl.when(c == 1)
+            def _():
+                gy.go(PLUS)
+
+            gy.relay_second(MINUS)
+
+            @pl.when(c == 1)
+            def _():
+                gy.go(FAR)
+                far_step(OWN)
+
+        @pl.when(t == 1)
+        def _():
+            gy.relay_second(PLUS)
+
+            @pl.when(c == 1)
+            def _():
+                far_step(MINUS)
+
+            gy.relay_second(FAR)
+
+        @pl.when(t == 2)
+        def _():
+            w_start()
+
+            @pl.when(c == 1)
+            def _():
+                far_step(PLUS)
+
+            @pl.when(c == 0)
+            def _():
+                far_step(OWN)
+                far_step(MINUS)
+
+        @pl.when(t == 3)
+        def _():
+            @pl.when(c == 0)
+            def _():
+                far_step(PLUS)
+
+            far_step(FAR)
+            w_relay()
+
+        gy.await_mate_row(t)
+        b = row_at(t)
+        project(dyf_ref, wo_v, dot_ref, b)
+        for k in range(ring):
+            @pl.when(b == k)
+            def _(k=k):
+                for i in range(k * tb // bq, (k + 1) * tb // bq):
+                    attend(i)
+        return 0
+
+    far_cp = {d: gy.push(gy.ref(d, FAR, c), gy.ref(d, FAR, c), gy.mate_recv.at[d, FAR], gy.mate) for d in range(4)}
+
+    def far_step(d):
+        for half in (0, 1):
+            gy.arrived(d, FAR, half)
+        far_cp[d].start()
+
+    lax.fori_loop(0, ring, turn, 0)
+
     for k in range(0, tokens, bq):
         ks = slice(k, k + bq)
         g_ref[ks, heads * e:(heads + 1) * e] = (dk_ref[:, ks] * scale).astype(BF16).T
         g_ref[ks, (heads + 1) * e:(heads + 2) * e] = dv_ref[:, ks].astype(BF16).T
     own_out.wait()
-    for cp in copies:
-        cp.wait()
-
-
-def _attention(ring, cores, heads, scale, qkvt, dot, wq):
-    tokens = qkvt.shape[1]
-    e = qkvt.shape[0] // (heads + 2)
+    w_finish()
+    gx.drain()
+    gy.drain()
+
+
+def _front(ring, cores, heads, scale, x, dy, w_in, wo):
+    rows, width = x.shape
+    tokens = rows * ring * ring * cores
+    hd = wo.shape[0]
+    e = hd // heads
     n_row = ring * cores
-    cw = wq.shape[1] // n_row
-    bq = min(256, tokens)
+    cw = width // n_row
+    bq = min(256, tokens // ring)
+    dma = pltpu.SemaphoreType.DMA
     return pl.pallas_call(
-        functools.partial(_attn_kernel, ring, cores, heads, scale, bq),
-        name="attn",
-        in_specs=[VMEM, VMEM, ANY],
-        out_specs=[VMEM, VMEM, VMEM, ANY],
+        functools.partial(_front_kernel, ring, cores, heads, scale, bq),
+        name="front",
+        in_specs=[ANY, ANY, ANY, ANY],
+        out_specs=[ANY, ANY, VMEM, VMEM, VMEM, ANY, ANY],
         out_shape=[
+            jax.ShapeDtypeStruct((tokens, width), BF16),
+            jax.ShapeDtypeStruct((tokens, width), BF16),
             jax.ShapeDtypeStruct((tokens, (heads + 2) * e), BF16),
-            jax.ShapeDtypeStruct((heads * e, tokens), BF16),
-            jax.ShapeDtypeStruct((heads * e, tokens), BF16),
-            jax.ShapeDtypeStruct((n_row, heads * e, cw), BF16),
+            jax.ShapeDtypeStruct((hd, tokens), BF16),
+            jax.ShapeDtypeStruct((hd, tokens), BF16),
+            jax.ShapeDtypeStruct((n_row, hd, cw), BF16),
+            jax.ShapeDtypeStruct((4, hd // 2, cw), BF16),
         ],
         scratch_shapes=[
+            pltpu.VMEM(w_in.shape, BF16),
+            pltpu.VMEM(wo.shape, BF16),
+            pltpu.VMEM((2, bq, width), BF16),
+            pltpu.VMEM((w_in.shape[0], tokens), BF16),
+            pltpu.VMEM((hd, tokens), BF16),
             pltpu.VMEM((bq, tokens), F32),
             pltpu.VMEM((e, tokens), F32),
             pltpu.VMEM((e, tokens), F32),
-            pltpu.VMEM((heads * e, cw), BF16),
-            pltpu.SemaphoreType.DMA((n_row,)),
-            pltpu.SemaphoreType.DMA((n_row,)),
-            pltpu.SemaphoreType.DMA((2,)),
+            pltpu.VMEM((hd, cw), BF16),
+            dma((2, 40)),
+            dma((2, 4, 4, 2)),
+            dma((2, 4, 4)),
+            dma((13,)),
+            dma((9,)),
+            dma((4,)),
+            dma((6,)),
+            dma((2,)),
         ],
-        compiler_params=pltpu.CompilerParams(collective_id=0, has_side_effects=True, vmem_limit_bytes=40 << 20),
-        cost_estimate=pl.CostEstimate(flops=12 * heads * tokens * tokens * e, bytes_accessed=8 << 20, transcendentals=heads * tokens * tokens // 2),
-    )(qkvt, dot, wq)
+        compiler_params=pltpu.CompilerParams(collective_id=0, has_side_effects=True, vmem_limit_bytes=56 << 20),
+        cost_estimate=pl.CostEstimate(flops=12 * heads * tokens * tokens * e, bytes_accessed=200 << 20, transcendentals=heads * tokens * tokens // 2),
+    )(x, dy, w_in, wo)
 
 
 def _grads_kernel(ring, cores, heads, g_ref, wrow_ref, wkv_ref, dqt_ref, ot_ref, x_ref, dy_ref,
@@ -506,13 +819,7 @@
         start = ((me // n_row) * kv_row, 0, lax.rem(me, n_row) * cw)
         wkv = jnp.concatenate([lax.dynamic_slice(w, start, (kv_row, e, cw)) for w in (wk, wv)], axis=1)
 
-        x_full = lax.all_gather(x_blk, "tp", axis=0, tiled=True)
-        dy_full = lax.all_gather(dy_blk, "tp", axis=0, tiled=True)
-        tokens = x_full.shape[0]
-        block = min(512, tokens)
-        qkvt = _proj(w_in, x_full, block)
-        dot = _proj(wo, dy_full, block)
-        g, dqt, ot, wrow = _attention(ring, cores, heads, scale, qkvt, dot, wq)
+        x_full, dy_full, g, dqt, ot, wrow, _ = _front(ring, cores, heads, scale, x_blk, dy_blk, w_in, wo)
         dx, dwq, dwo, dwk, dwv = _grads(ring, cores, heads, g, wrow, wkv, dqt, ot, x_full, dy_full)
         return (dx, jnp.transpose(dwq.reshape(heads, e, model_dim), (2, 0, 1)), dwo.reshape(heads, e, model_dim), dwk.T, dwv.T)
 

time: 472 us -> 400 us (0.85)
  waiting for transfers between devices: 199 us -> 0 us
  Pallas kernels: 226 us -> 373 us
  between operations: 14.2 us -> 0.74 us
  local copies, waits for them, and re-layouts: 25.5 us -> 18.2 us
    all_gather x2 -> x0, waiting for transfers between devices: 197 us -> none  [the longest x1 104 us: local_grads(): dy_full = lax.all_gather(dy_blk, 'tp', axis=0, tiled=True)]
    pallas_call x3 -> x1, Pallas kernels: 104 us -> 253 us  [_front(): pl.pallas_call(functools.partial(_front_kernel, ring, cores, heads, scale...]
    unnamed x25 -> x15, local copies, waits for them, and re-layouts: 22.5 us -> 15.3 us
  transfers between devices with their start and end apart: 2 -> 0, of which waited for: 2 -> 0; matrix products, arithmetic and copies ran while one was open for 2% -> 0% of each run, Pallas kernels for 3% -> 0%
where the time goes in v2:
time: 400 us; the launch traced here: 399 us
  Pallas kernels  373 us (93%)
  local copies, waits for them, and re-layouts  18.2 us (5%)
  other arithmetic  6.6 us (2%)
    pallas_call x1, Pallas kernels, _front(): pl.pallas_call(functools.partial(_front_kernel, ring, cores, heads, scale...  253 us
    pallas_call x1, Pallas kernels, _grads(): pl.pallas_call(functools.partial(_grads_kernel, ring, cores, heads), name...  120 us
    unnamed x15, local copies, waits for them, and re-layouts  15.3 us

profile of v2, /device:TPU:97, one launch (start us, length us, event | category | flops | bytes accessed | tf_op | source)
XLA Modules:
  0.0 398.9 jit_solution(890319111457463024)
XLA Ops:
  0.7 0.0 copy-start
  0.7 1.2 dynamic-slice_bitcast_fusion.2
  1.9 0.8 pad_maximum_fusion.1.wkv_ref
  2.7 1.7 dynamic-slice_bitcast_fusion
  4.5 0.0 copy-done
  4.5 5.8 %pad_maximum_fusion.w_ref = bf16[384,8192]{1,0:T(8,128)(2,1)} fusion(bf16[64,8192]{1,0:T(8,128)(2,1)S(1)} %get-tuple-element.27, bf16[64,8192]{1,0:T(8,128)(2,1)S(1)} %get-tuple-element.28, bf16[256,8192]{1,0:T(8,128)(2,1)S(1)} %bitcast.26), kind=kLoop, calls=%fused_computation | loop fusion | flops 18874368 | bytes 12582912 | tf_op jit(solution)/shard_map/concatenate | solution.py:816
  10.2 253.3 %front.1 = (bf16[2048,8192]{1,0:T(8,128)(2,1)}, bf16[2048,8192]{1,0:T(8,128)(2,1)}, bf16[2048,384]{1,0:T(8,128)(2,1)}, bf16[256,2048]{1,0:T(8,128)(2,1)}, bf16[2...) custom-call(bf16[64,8192]{1,0:T(8,128)(2,1)} %x_ref.1, bf16[64,8192]{1,0:T(8,128)(2,1)} %dy_ref.1, ...), custom_call_target="tpu_custom_call" | custom-call | flops 12884901888 | bytes 209715200 | tf_op jit(solution)/shard_map/front/pallas_call | solution.py:481
  263.5 120.1 %grads.1 = (bf16[64,8192]{1,0:T(8,128)(2,1)}, f32[256,8192]{1,0:T(8,128)}, f32[256,8192]{1,0:T(8,128)}, f32[64,2048]{1,0:T(8,128)}, f32[64,2048]{1,0:T(8,128)}) custom-call(bf16[2048,384]{1,0:T(8,128)(2,1)} %get-tuple-element.16.g_ref, bf16[8,256,1024]{2,1,0:T(8,128)(2,1)} %get-tuple-element.17.wrow_ref, bf16[2,128,1024]{2,1,0:T(8,128)(2,1)} %pad_maximum_fusion.1.wkv_ref, ...), custom_call_target="tpu_custom_call" | custom-call | flops 38654705664 | bytes 104857600 | tf_op jit(solution)/shard_map/grads/pallas_call | solution.py:760
  383.6 0.0 slice-start
  383.7 2.4 copy.16
  386.1 0.0 slice-start.1
  386.1 7.8 %copy.17 = f32[8192,4,64]{0,2,1:T(8,128)} copy(f32[8192,4,64]{0,2,1:T(8,128)} %bitcast.25) | data formatting | bytes 16777216
  393.9 0.0 slice-done
  393.9 0.0 slice-done.1
  393.9 0.0 copy-start.2
  393.9 0.0 copy-start.1
  393.9 3.4 copy.18
  397.3 0.0 copy-done.2
  397.3 0.8 copy.19
  398.1 0.0 copy-done.1
  398.1 0.8 copy.20
  (1 shorter events, 0.0 us)
Async XLA Ops:
  0.7 3.8 copy-start
  383.6 10.3 %slice-start = ((s8[8388608]{0:T(1024)(128)(4,1)}), s8[4194304]{0:T(1024)(128)(4,1)S(1)}, s32[]{:S(2)}) async-start(s8[8388608]{0:T(1024)(128)(4,1)} %bitcast.22), calls=%async_computation | async-start | bytes 8388608
  386.1 7.8 %slice-start.1 = ((s8[8388608]{0:T(1024)(128)(4,1)}), s8[4194304]{0:T(1024)(128)(4,1)S(1)}, s32[]{:S(2)}) async-start(s8[8388608]{0:T(1024)(128)(4,1)} %bitcast.22), calls=%async_computation.1 | async-start | bytes 8388608
  393.9 3.4 copy-start.2
  393.9 4.2 %copy-start.1 = (f32[64,2048]{1,0:T(8,128)S(1)}, f32[64,2048]{1,0:T(8,128)}, u32[]{:S(2)}) copy-start(f32[64,2048]{1,0:T(8,128)} %get-tuple-element.26) | copy-start | bytes 1572868

commit v3 on v2

--- a/solution.py
+++ b/solution.py
@@ -165,9 +165,9 @@
             _remote(ref, ref, self.send.at[k], self.send.at[k], self.mate).wait_send()
 
 
-def _front_kernel(ring, cores, heads, scale, bq, x_ref, dy_ref, w_ref, wo_ref,
+def _front_kernel(ring, cores, heads, scale, bq, bs, x_ref, dy_ref, w_ref, wk_ref, wv_ref, wo_ref,
                   xf_ref, dyf_ref, g_ref, dqt_ref, ot_ref, wrow_ref, hop_ref,
-                  w_v, wo_v, xblk, qkvt_ref, dot_ref, s_ref, dk_ref, dv_ref, w_buf,
+                  w_v, wo_v, xblk, qkvt_ref, dot_ref, s_ref, dp_ref, dk_ref, dv_ref, w_buf,
                   send, recv, mate_recv, w_send, w_recv, hop_recv, ld_sem, blk_sem):
     at = Place(ring, cores)
     n_row = at.n_row
@@ -180,7 +180,13 @@
     gx = Gather(at, x_ref, xf_ref, send.at[0], recv.at[0], mate_recv.at[0])
     gy = Gather(at, dy_ref, dyf_ref, send.at[1], recv.at[1], mate_recv.at[1])
 
-    loads = [pltpu.make_async_copy(w_ref, w_v, ld_sem.at[0]), pltpu.make_async_copy(wo_ref, wo_v, ld_sem.at[1])]
+    kv = (at.y * n_row + at.r) // (n_row * ring // wk_ref.shape[0])
+    loads = [
+        pltpu.make_async_copy(w_ref, w_v.at[pl.ds(0, hd), :], ld_sem.at[0]),
+        pltpu.make_async_copy(wo_ref, wo_v, ld_sem.at[1]),
+        pltpu.make_async_copy(wk_ref.at[kv], w_v.at[pl.ds(hd, e), :], ld_sem.at[6]),
+        pltpu.make_async_copy(wv_ref.at[kv], w_v.at[pl.ds(hd + e, e), :], ld_sem.at[7]),
+    ]
     rows = x_ref.shape[0]
     own_rows = pl.ds(pl.multiple_of((at.y * n_row + at.r) * rows, rows), rows)
     ins = [pltpu.make_async_copy(src, xblk.at[i, pl.ds(0, rows), :], ld_sem.at[2 + i]) for i, src in enumerate((x_ref, dy_ref))]
@@ -274,63 +280,70 @@
     lax.fori_loop(0, ring, x_turn, 0)
 
     krow, vrow = heads * e, (heads + 1) * e
-    row = lax.broadcasted_iota(jnp.int32, (bq, bq), 0)
-    col = lax.broadcasted_iota(jnp.int32, (bq, bq), 1)
-
-    def attend(i):
-        q0 = i * bq
-        chunks = [slice(k, k + bq) for k in range(0, q0 + bq, bq)]
-        qs = slice(q0, q0 + bq)
-
-        def head(h, _):
-            hs = pl.ds(pl.multiple_of(h * e, e), e)
-            qt = qkvt_ref[hs, qs]
-            dot = dot_ref[hs, qs]
+    keys_k, keys_v = slice(krow, krow + e), slice(vrow, vrow + e)
+    m4 = heads * bs
+    row = lax.broadcasted_iota(jnp.int32, (m4, bq), 0) & (bs - 1)
+    col = lax.broadcasted_iota(jnp.int32, (m4, bq), 1)
+
+    def lanes(v):
+        parts = [v[:, t:t + 128] for t in range(0, v.shape[1], 128)]
+        return parts
+
+    def attend(k):
+        base = k * tb
+        chunks = [slice(t, t + bq) for t in range(0, base + tb, bq)]
+
+        def queries(j, _):
+            q0 = pl.multiple_of(base + j * bs, bs)
+            qs = pl.ds(q0, bs)
+            qt = jnp.concatenate([qkvt_ref[h * e:(h + 1) * e, qs] for h in range(heads)], axis=1)
+            dot = jnp.concatenate([dot_ref[h * e:(h + 1) * e, qs] for h in range(heads)], axis=1)
             q = qt.T
             do = dot.T
             m = None
             for ks in chunks:
-                s = _nn(q, qkvt_ref[krow:krow + e, ks])
-                if ks.start == q0:
-                    s = jnp.where(row >= col, s, -jnp.inf)
+                s = _nn(q, qkvt_ref[keys_k, ks])
+                if ks.start >= base:
+                    s = jnp.where(col + (ks.start - base) <= row + j * bs, s, -jnp.inf)
                 s_ref[:, ks] = s
-                part = s[:, :128]
-                for t in range(128, bq, 128):
-                    part = jnp.maximum(part, s[:, t:t + 128])
-                m = part if m is None else jnp.maximum(m, part)
+                for part in lanes(s):
+                    m = part if m is None else jnp.maximum(m, part)
             m = jnp.max(m, axis=1, keepdims=True)
             total = None
             for ks in chunks:
                 p = jnp.exp2((s_ref[:, ks] - m) * (scale * LOG2E))
                 s_ref[:, ks] = p
-                part = p[:, :128]
-                for t in range(128, bq, 128):
-                    part = part + p[:, t:t + 128]
-                total = part if total is None else total + part
+                for part in lanes(p):
+                    total = part if total is None else total + part
+                dp_ref[:, ks] = _nn(do, qkvt_ref[keys_v, ks])
             inv = 1.0 / jnp.sum(total, axis=1, keepdims=True)
             out = None
             for ks in chunks:
                 p = s_ref[:, ks] * inv
                 s_ref[:, ks] = p
                 pb = p.astype(BF16)
-                part = _nt(pb, qkvt_ref[vrow:vrow + e, ks])
+                part = _nt(qkvt_ref[keys_v, ks], pb)
                 out = part if out is None else out + part
                 dv_ref[:, ks] += _nn(dot, pb)
             out = out.astype(BF16)
-            ot_ref[hs, qs] = out.T
-            delta = jnp.sum(do.astype(F32) * out.astype(F32), axis=1, keepdims=True)
+            delta = jnp.sum(dot.astype(F32) * out.astype(F32), axis=0, keepdims=True)
+            delta = jnp.broadcast_to(delta, (128, m4)).T[:, :1]
             dq = None
             for ks in chunks:
-                dp = _nn(do, qkvt_ref[vrow:vrow + e, ks])
-                ds = (s_ref[:, ks] * (dp - delta)).astype(BF16)
-                part = _nt(ds, qkvt_ref[krow:krow + e, ks])
+                ds = (s_ref[:, ks] * (dp_ref[:, ks] - delta)).astype(BF16)
+                part = _nt(qkvt_ref[keys_k, ks], ds)
                 dq = part if dq is None else dq + part
                 dk_ref[:, ks] += _nn(qt, ds)
-            dqt_ref[hs, qs] = (dq * scale).astype(BF16).T
+            dq = (dq * scale).astype(BF16)
+            for h in range(heads):
+                ot_ref[h * e:(h + 1) * e, qs] = out[:, h * bs:(h + 1) * bs]
+                dqt_ref[h * e:(h + 1) * e, qs] = dq[:, h * bs:(h + 1) * bs]
+            for h in range(0, heads, 2):
+                pair = jnp.concatenate([dq[:, h * bs:(h + 1) * bs], dq[:, (h + 1) * bs:(h + 2) * bs]], axis=0)
+                g_ref[qs, h * e:(h + 2) * e] = pair.T
             return 0
 
-        lax.fori_loop(0, heads, head, 0)
-        g_ref[qs, 0:heads * e] = dqt_ref[:, qs].T
+        lax.fori_loop(0, tb // bs, queries, 0)
 
     hh = hd // 2
 
@@ -446,8 +459,7 @@
         for k in range(ring):
             @pl.when(b == k)
             def _(k=k):
-                for i in range(k * tb // bq, (k + 1) * tb // bq):
-                    attend(i)
+                attend(k)
         return 0
 
     far_cp = {d: gy.push(gy.ref(d, FAR, c), gy.ref(d, FAR, c), gy.mate_recv.at[d, FAR], gy.mate) for d in range(4)}
@@ -469,7 +481,7 @@
     gy.drain()
 
 
-def _front(ring, cores, heads, scale, x, dy, w_in, wo):
+def _front(ring, cores, heads, scale, x, dy, wq, wk, wv, wo):
     rows, width = x.shape
     tokens = rows * ring * ring * cores
     hd = wo.shape[0]
@@ -477,11 +489,12 @@
     n_row = ring * cores
     cw = width // n_row
     bq = min(256, tokens // ring)
+    bs = min(128, tokens // ring)
     dma = pltpu.SemaphoreType.DMA
     return pl.pallas_call(
-        functools.partial(_front_kernel, ring, cores, heads, scale, bq),
+        functools.partial(_front_kernel, ring, cores, heads, scale, bq, bs),
         name="front",
-        in_specs=[ANY, ANY, ANY, ANY],
+        in_specs=[ANY] * 6,
         out_specs=[ANY, ANY, VMEM, VMEM, VMEM, ANY, ANY],
         out_shape=[
             jax.ShapeDtypeStruct((tokens, width), BF16),
@@ -493,12 +506,13 @@
             jax.ShapeDtypeStruct((4, hd // 2, cw), BF16),
         ],
         scratch_shapes=[
-            pltpu.VMEM(w_in.shape, BF16),
+            pltpu.VMEM((hd + 2 * e, width), BF16),
             pltpu.VMEM(wo.shape, BF16),
             pltpu.VMEM((2, bq, width), BF16),
-            pltpu.VMEM((w_in.shape[0], tokens), BF16),
+            pltpu.VMEM((hd + 2 * e, tokens), BF16),
             pltpu.VMEM((hd, tokens), BF16),
-            pltpu.VMEM((bq, tokens), F32),
+            pltpu.VMEM((heads * bs, tokens), F32),
+            pltpu.VMEM((heads * bs, tokens), F32),
             pltpu.VMEM((e, tokens), F32),
             pltpu.VMEM((e, tokens), F32),
             pltpu.VMEM((hd, cw), BF16),
@@ -508,15 +522,15 @@
             dma((13,)),
             dma((9,)),
             dma((4,)),
-            dma((6,)),
+            dma((8,)),
             dma((2,)),
         ],
         compiler_params=pltpu.CompilerParams(collective_id=0, has_side_effects=True, vmem_limit_bytes=56 << 20),
         cost_estimate=pl.CostEstimate(flops=12 * heads * tokens * tokens * e, bytes_accessed=200 << 20, transcendentals=heads * tokens * tokens // 2),
-    )(x, dy, w_in, wo)
-
-
-def _grads_kernel(ring, cores, heads, g_ref, wrow_ref, wkv_ref, dqt_ref, ot_ref, x_ref, dy_ref,
+    )(x, dy, wq, wk, wv, wo)
+
+
+def _grads_kernel(ring, cores, heads, g_ref, wrow_ref, wk_ref, wv_ref, dqt_ref, ot_ref, x_ref, dy_ref,
                   dx_ref, dwq_ref, dwo_ref, dwk_ref, dwv_ref,
                   gq, w_all, part, rs_half, rs_full, stage, xbuf, obuf, kvt,
                   ag_send, ag_recv, rs_send, rs_recv, out_send, out_recv, in_sem, o_sem, ld_sem):
@@ -532,16 +546,19 @@
     cw = w_all.shape[1]
     hw = cw // 2
     half_a, half_b = pl.ds(0, hw), pl.ds(hw, hw)
-    n_ld = 2 * n_row + 1
 
     def gcols(slot):
         return pl.ds(pl.multiple_of(slot * gw, gw), gw)
 
     loads = [pltpu.make_async_copy(g_ref, gq.at[:, gcols(at.r)], ld_sem.at[0])]
-    per_kv = n_row // wkv_ref.shape[0]
+    n_kv = wk_ref.shape[0] // ring
+    per_kv = n_row // n_kv
+    own_cols = pl.ds(pl.multiple_of(at.r * cw, cw), cw)
     for r in range(n_row):
-        loads.append(pltpu.make_async_copy(wrow_ref.at[r], w_all.at[pl.ds(r * gw, hd), :], ld_sem.at[1 + r]))
-        loads.append(pltpu.make_async_copy(wkv_ref.at[r // per_kv], w_all.at[pl.ds(r * gw + hd, gw - hd), :], ld_sem.at[1 + n_row + r]))
+        kv = at.y * n_kv + r // per_kv
+        loads.append(pltpu.make_async_copy(wrow_ref.at[r], w_all.at[pl.ds(r * gw, hd), :], ld_sem.at[1 + 3 * r]))
+        loads.append(pltpu.make_async_copy(wk_ref.at[kv, :, own_cols], w_all.at[pl.ds(r * gw + hd, e), :], ld_sem.at[2 + 3 * r]))
+        loads.append(pltpu.make_async_copy(wv_ref.at[kv, :, own_cols], w_all.at[pl.ds(r * gw + hd + e, e), :], ld_sem.at[3 + 3 * r]))
     for cp in loads:
         cp.start()
 
@@ -688,7 +705,6 @@
     partial(3)
     stream(x_ref, dqt_ref, dwq_ref, cut[2], cut[4])
 
-    n_kv = wkv_ref.shape[0]
     first = (at.r // per_kv) * per_kv
     for q in range(per_kv):
         cols = pl.ds(pl.multiple_of((first + q) * gw + hd, 128), gw - hd)
@@ -746,7 +762,7 @@
         cp.wait_send()
 
 
-def _grads(ring, cores, heads, g, wrow, wkv, dqt, ot, x, dy):
+def _grads(ring, cores, heads, g, wrow, wk, wv, dqt, ot, x, dy):
     tokens, width = x.shape
     n_row = ring * cores
     hd = dqt.shape[0]
@@ -754,13 +770,13 @@
     gw = g.shape[1]
     tb = tokens // ring
     cw = width // n_row
-    per_kv = n_row // wkv.shape[0]
+    per_kv = n_row * ring // wk.shape[0]
     bc = min(512, cw // 2)
     dma = pltpu.SemaphoreType.DMA
     return pl.pallas_call(
         functools.partial(_grads_kernel, ring, cores, heads),
         name="grads",
-        in_specs=[ANY, ANY, ANY, VMEM, VMEM, ANY, ANY],
+        in_specs=[ANY, ANY, ANY, ANY, VMEM, VMEM, ANY, ANY],
         out_specs=[ANY, ANY, ANY, VMEM, VMEM],
         out_shape=[
             jax.ShapeDtypeStruct((tb // n_row, width), BF16),
@@ -787,11 +803,11 @@
             dma((n_row,)),
             dma((2,)),
             dma((2,)),
-            dma((2 * n_row + 1,)),
+            dma((3 * n_row + 1,)),
         ],
         compiler_params=pltpu.CompilerParams(collective_id=1, has_side_effects=True, vmem_limit_bytes=60 << 20),
         cost_estimate=pl.CostEstimate(flops=2 * tokens * width * (n_row * gw // n_row + 3 * hd), bytes_accessed=100 << 20, transcendentals=0),
-    )(g, wrow, wkv, dqt, ot, x, dy)
+    )(g, wrow, wk, wv, dqt, ot, x, dy)
 
 
 def solution(mesh):
@@ -805,22 +821,13 @@
         model_dim, kv_heads, e = w_k.shape
         heads = wq_loc.shape[1]
         hd = heads * e
-        n_row = ring * cores
         scale = e ** -0.5
-        me = lax.axis_index("tp")
         wq = jnp.transpose(wq_loc, (1, 2, 0)).reshape(hd, model_dim)
         wk = jnp.transpose(w_k, (1, 2, 0))
         wv = jnp.transpose(w_v, (1, 2, 0))
         wo = wo_loc.reshape(hd, model_dim)
-        j = me // (n // kv_heads)
-        w_in = jnp.concatenate([wq, lax.dynamic_index_in_dim(wk, j, 0, False), lax.dynamic_index_in_dim(wv, j, 0, False)])
-        kv_row = kv_heads // ring
-        cw = model_dim // n_row
-        start = ((me // n_row) * kv_row, 0, lax.rem(me, n_row) * cw)
-        wkv = jnp.concatenate([lax.dynamic_slice(w, start, (kv_row, e, cw)) for w in (wk, wv)], axis=1)
-
-        x_full, dy_full, g, dqt, ot, wrow, _ = _front(ring, cores, heads, scale, x_blk, dy_blk, w_in, wo)
-        dx, dwq, dwo, dwk, dwv = _grads(ring, cores, heads, g, wrow, wkv, dqt, ot, x_full, dy_full)
+        x_full, dy_full, g, dqt, ot, wrow, _ = _front(ring, cores, heads, scale, x_blk, dy_blk, wq, wk, wv, wo)
+        dx, dwq, dwo, dwk, dwv = _grads(ring, cores, heads, g, wrow, wk, wv, dqt, ot, x_full, dy_full)
         return (dx, jnp.transpose(dwq.reshape(heads, e, model_dim), (2, 0, 1)), dwo.reshape(heads, e, model_dim), dwk.T, dwv.T)
 
     tok = P(("dp", "tp"))

time: 400 us -> 379 us (0.948)
  Pallas kernels: 373 us -> 362 us
  other arithmetic: 6.6 us -> 0.01 us
    pallas_call x1, Pallas kernels: 253 us -> 241 us  [_front(): pl.pallas_call(functools.partial(_front_kernel, ring, cores, heads, scale...]
    concatenate x2 -> x0, other arithmetic: 6.6 us -> none  [the longest x1 5.77 us: local_grads(): jnp.concatenate([wq, lax.dynamic_index_in_dim(wk, j, 0, False), lax.dynam...]
    unnamed x15 -> x13, local copies, waits for them, and re-layouts: 15.3 us -> 15.3 us
where the time goes in v3:
time: 379 us; the launch traced here: 378 us
  Pallas kernels  362 us (96%)
  local copies, waits for them, and re-layouts  15.3 us (4%)
    pallas_call x1, Pallas kernels, _front(): pl.pallas_call(functools.partial(_front_kernel, ring, cores, heads, scale...  241 us
    pallas_call x1, Pallas kernels, _grads(): pl.pallas_call(functools.partial(_grads_kernel, ring, cores, heads), name...  120 us
    unnamed x13, local copies, waits for them, and re-layouts  15.3 us

profile of v3, /device:TPU:97, one launch (start us, length us, event | category | flops | bytes accessed | tf_op | source)
XLA Modules:
  0.0 377.6 jit_solution(7374416315893329594)
XLA Ops:
  0.6 241.4 %front.1 = (bf16[2048,8192]{1,0:T(8,128)(2,1)}, bf16[2048,8192]{1,0:T(8,128)(2,1)}, bf16[2048,384]{1,0:T(8,128)(2,1)}, bf16[256,2048]{1,0:T(8,128)(2,1)}, bf16[2...) custom-call(bf16[64,8192]{1,0:T(8,128)(2,1)} %x_ref.1, bf16[64,8192]{1,0:T(8,128)(2,1)} %dy_ref.1, ...), custom_call_target="tpu_custom_call" | custom-call | flops 12884901888 | bytes 209715200 | tf_op jit(solution)/shard_map/front/pallas_call | solution.py:494
  242.1 120.2 %grads.1 = (bf16[64,8192]{1,0:T(8,128)(2,1)}, f32[256,8192]{1,0:T(8,128)}, f32[256,8192]{1,0:T(8,128)}, f32[64,2048]{1,0:T(8,128)}, f32[64,2048]{1,0:T(8,128)}) custom-call(bf16[2048,384]{1,0:T(8,128)(2,1)} %get-tuple-element.16.g_ref, bf16[8,256,1024]{2,1,0:T(8,128)(2,1)} %get-tuple-element.17.wrow_ref, bf16[8,64,8192]{2,1,0:T(8,128)(2,1)} %bitcast.19, ...), custom_call_target="tpu_custom_call" | custom-call | flops 38654705664 | bytes 104857600 | tf_op jit(solution)/shard_map/grads/pallas_call | solution.py:776
  362.3 0.0 slice-start
  362.3 2.4 copy.16
  364.7 0.0 slice-start.1
  364.7 7.8 %copy.17 = f32[8192,4,64]{0,2,1:T(8,128)} copy(f32[8192,4,64]{0,2,1:T(8,128)} %bitcast.15) | data formatting | bytes 16777216
  372.6 0.0 slice-done
  372.6 0.0 slice-done.1
  372.6 0.0 copy-start.1
  372.6 0.0 copy-start
  372.6 3.4 copy.18
  376.0 0.0 copy-done.1
  376.0 0.8 copy.19
  376.8 0.0 copy-done
  376.8 0.8 copy.20
  (1 shorter events, 0.0 us)
Async XLA Ops:
  362.3 10.3 %slice-start = ((s8[8388608]{0:T(1024)(128)(4,1)}), s8[4194304]{0:T(1024)(128)(4,1)S(1)}, s32[]{:S(2)}) async-start(s8[8388608]{0:T(1024)(128)(4,1)} %bitcast.12), calls=%async_computation | async-start | bytes 8388608
  364.7 7.8 %slice-start.1 = ((s8[8388608]{0:T(1024)(128)(4,1)}), s8[4194304]{0:T(1024)(128)(4,1)S(1)}, s32[]{:S(2)}) async-start(s8[8388608]{0:T(1024)(128)(4,1)} %bitcast.12), calls=%async_computation.1 | async-start | bytes 8388608
  372.6 3.4 copy-start.1
  372.6 4.2 %copy-start = (f32[64,2048]{1,0:T(8,128)S(1)}, f32[64,2048]{1,0:T(8,128)}, u32[]{:S(2)}) copy-start(f32[64,2048]{1,0:T(8,128)} %get-tuple-element.26) | copy-start | bytes 1572868
